TPU v7x, 32 devices: a whole 2x2x4 slice. The times are simulated.
32 devices in a mesh: pipe: 2 (over core), seq: 8 (over z, x), tp: 2 (over y).
Axes of the slice: x: 2, y: 2, z: 4, core: 2. Of those that a mesh axis runs over, the one named last changes fastest.
Arguments:
- hidden_in: bfloat16 [1, 4096, 2560], P(None, ('seq', 'tp')), may hold values from -6 to 6
- doc_ids: int32 [1, 4096], P(None, 'seq'), may hold values from 0 to 1, never falling along the last dimension, each value on 1 to 3072 neighbouring positions
- norm_gain: float32 [2, 2560], P('pipe'), may hold values from 0.1 to 1.9
- in_zx: bfloat16 [2, 2560, 2, 5120], P('pipe', None, None, 'tp'), may hold values from -0.125 to 0.125
- in_bc: bfloat16 [2, 2560, 256], P('pipe'), may hold values from -0.125 to 0.125
- in_dt: bfloat16 [2, 2560, 80], P('pipe', None, 'tp'), may hold values from -0.125 to 0.125
- conv_x: float32 [2, 4, 5120], P('pipe', None, 'tp'), may hold values from -3 to 3
- conv_bc: float32 [2, 4, 256], P('pipe'), may hold values from -3 to 3
- bias_x: float32 [2, 5120], P('pipe', 'tp'), may hold values from -3 to 3
- bias_bc: float32 [2, 256], P('pipe'), may hold values from -3 to 3
- dt_bias: float32 [2, 80], P('pipe', 'tp'), may hold values from -2 to 1
- a_log: float32 [2, 80], P('pipe', 'tp'), may hold values from -12 to 0, as said below
- d_skip: float32 [2, 80], P('pipe', 'tp'), may hold values from 0.5 to 1.5
- gated_gain: float32 [2, 5120], P('pipe', 'tp'), may hold values from 0.1 to 1.9
- out_w: bfloat16 [2, 5120, 2560], P('pipe', 'tp'), may hold values from -0.078125 to 0.078125
Outputs:
- section_out: bfloat16 [2, 1, 4096, 2560], P('pipe', None, ('seq', 'tp'))
Inputs may be any that keep to these rules, and one draw needn't show every extreme that they name: `doc_ids`: in each row the document numbers start at 0, never fall, and rise by one where a new document begins; every document spans 1 to 3072 positions. `a_log`: logarithms of rates between 0.5 / 4096 and 1.
All inputs are finite; a program needn't handle non-finite values.
Results may differ from a plain program's by a relative error of at most 0.02.
Values may be sent and summed in bfloat16 or wider, within the bound.
A program may use at most 192 MiB of HBM per device.

v0:
```python
import functools

import jax
import jax.numpy as jnp
from jax import lax
from jax.experimental import pallas as pl
from jax.experimental.pallas import tpu as pltpu
from jax.sharding import PartitionSpec as P

epsilon = 1e-05
LOG2E = 1.4426950408889634
HALO = 16
CHUNK = 128
LANES = 128
MESH = pl.DeviceIdType.MESH
f32 = jnp.float32
bf16 = jnp.bfloat16


def live_shift(block, axis, distance, live, wrap=False):
    size = lax.axis_size(axis)
    route = []
    for i in range(size):
        j = i + distance
        if wrap or j < size:
            route.append((live * size + i, live * size + j % size))
    return lax.ppermute(block, ("pipe", axis), route)


def gathered_rows(rows, axis, live):
    size = lax.axis_size(axis)
    place = lax.axis_index(axis)
    count = rows.shape[0]
    whole = jnp.zeros((size * count,) + rows.shape[1:], rows.dtype)
    whole = lax.dynamic_update_slice_in_dim(whole, rows, place * count, 0)
    for step in range(1, size):
        other = live_shift(rows, axis, step, live, True)
        source = lax.rem(place - step + size, size)
        whole = lax.dynamic_update_slice_in_dim(whole, other, source * count, 0)
    return whole


def scattered_sum(rows, squares, axis, live):
    size = lax.axis_size(axis)
    place = lax.axis_index(axis)
    count = rows.shape[0] // size
    total = lax.dynamic_slice_in_dim(rows, place * count, count, 0)
    square = lax.dynamic_slice_in_dim(squares, place * count, count, 0)
    for step in range(1, size):
        target = lax.rem(place + step, size)
        piece = lax.dynamic_slice_in_dim(rows, target * count, count, 0).astype(bf16)
        term = lax.dynamic_slice_in_dim(squares, target * count, count, 0)
        total = total + live_shift(piece, axis, step, live, True).astype(f32)
        square = square + live_shift(term, axis, step, live, True)
    return total, square


def silu(value):
    half = 0.5 * value
    return half + half * jnp.tanh(half)


def split_pair(value):
    high = value.astype(bf16)
    low = (value - high.astype(f32)).astype(bf16)
    return jnp.concatenate([high, low], 1)


def mixer_kernel(
    live,
    zx_ref,
    bcdt_ref,
    idc_ref,
    idr_ref,
    wx_ref,
    wbc_ref,
    hv_ref,
    g_ref,
    ss_ref,
    mask_s,
    l_s,
    m_s,
    lg_s,
    ew_s,
    cw_s,
    keep_s,
    b_s,
    c_s,
    gm_s,
    xc_s,
    fresh_s,
    y_s,
    send_s,
    recv_s,
    ksend_s,
    krecv_s,
    back_s,
    inc_s,
    send_sem,
    recv_sem,
    ksend_sem,
    krecv_sem,
    bsend_sem,
    brecv_sem,
):
    size = lax.axis_size("seq")
    me = lax.axis_index("seq")
    rows = g_ref.shape[0]
    width = g_ref.shape[1]
    chunks = rows // CHUNK
    tiles = width // LANES
    states = b_s.shape[1]
    slab = states // size
    heads_pad = hv_ref.shape[1]
    head_width = LANES // 2

    def lane_iota(shape):
        return lax.broadcasted_iota(jnp.int32, shape, 1)

    def row_iota(shape):
        return lax.broadcasted_iota(jnp.int32, shape, 0)

    def selector(tile, count, dtype):
        shape = (count, LANES)
        hit = lax.rem(row_iota(shape), heads_pad) == tile * 2 + lane_iota(shape) // head_width
        return hit.astype(f32).astype(dtype)

    def hop(source, target_ref, distance, send, recv):
        return pltpu.make_async_remote_copy(
            src_ref=source,
            dst_ref=target_ref,
            send_sem=send.at[distance - 1],
            recv_sem=recv.at[distance - 1],
            device_id={"seq": lax.rem(me + distance, size)},
            device_id_type=MESH,
        )

    @pl.when(lax.axis_index("pipe") == live)
    def _():
        barrier = pltpu.get_barrier_semaphore()
        for distance in range(1, size):
            pl.semaphore_signal(
                barrier,
                inc=1,
                device_id={"seq": lax.rem(me + distance, size)},
                device_id_type=MESH,
            )

        square_shape = (CHUNK, CHUNK)
        lower = row_iota(square_shape) >= lane_iota(square_shape)
        lower_f = lower.astype(f32)

        @pl.loop(0, chunks)
        def _(k):
            base = pl.multiple_of(k * CHUNK, CHUNK)
            here = pl.ds(base, CHUNK)
            ids_ext = idc_ref[pl.ds(base, CHUNK + HALO), :]
            seg = ids_ext[HALO:]
            prev = ids_ext[HALO - 1 : HALO]
            last = ids_ext[HALO + CHUNK - 1 :]
            for d in range(1, 4):
                same = pltpu.roll(ids_ext, d, 0)[HALO:] == seg
                mask_s[d - 1, here, :] = same.astype(f32)
            raw = bcdt_ref[pl.ds(base + HALO, CHUNK), 2 * states :] + hv_ref[0:1, :]
            step = jnp.maximum(raw, 0.0) + jnp.log1p(jnp.exp(-jnp.abs(raw)))
            level = jnp.dot(
                lower_f,
                step * hv_ref[1:2, :],
                precision=lax.Precision.HIGHEST,
                preferred_element_type=f32,
            )
            l_s[here, :] = level
            step_log = jnp.log(step) * LOG2E
            m_s[k] = (level - step_log).T
            lg_s[k] = step_log.T
            end = level[CHUNK - 1 :]
            ew_s[here, :] = split_pair(
                jnp.exp2(end - level) * step * (seg == last).astype(f32)
            )
            cw_s[here, :] = split_pair(jnp.exp2(level) * (seg == prev).astype(f32))
            keep_s[k] = jnp.broadcast_to(jnp.exp2(end) * (last == prev).astype(f32), (8, heads_pad))
            for half in range(2):
                cols = pl.ds(half * states, states)
                wide = bcdt_ref[pl.ds(base, CHUNK + HALO), cols]
                total = wbc_ref[4:5, cols] + wbc_ref[3:4, cols] * wide[HALO:]
                for d in range(1, 4):
                    total += (
                        mask_s[d - 1, here, :]
                        * wbc_ref[3 - d : 4 - d, cols]
                        * pltpu.roll(wide, d, 0)[HALO:]
                    )
                place = b_s if half == 0 else c_s
                place[here, :] = silu(total).astype(bf16)
            gram = lax.dot_general(
                c_s[here, :], b_s[here, :], (((1,), (1,)), ((), ())), preferred_element_type=f32
            )
            same_doc = seg == idr_ref[0:1, pl.ds(base, CHUNK)]
            gm_s[k] = jnp.where(lower & same_doc, gram, 0.0)

        @pl.loop(0, tiles)
        def _(tile):
            lanes = pl.ds(pl.multiple_of(tile * LANES, LANES), LANES)
            x_lanes = pl.ds(pl.multiple_of(width + tile * LANES, LANES), LANES)
            pick = selector(tile, 2 * heads_pad, bf16)
            pick_f = selector(tile, heads_pad, f32)
            state = jnp.zeros((states, LANES), f32)
            keep_all = jnp.ones((8, LANES), f32)
            for k in range(chunks):
                here = pl.ds(k * CHUNK, CHUNK)
                wide = zx_ref[pl.ds(k * CHUNK, CHUNK + HALO), x_lanes].astype(f32)
                total = wx_ref[4:5, lanes] + wx_ref[3:4, lanes] * wide[HALO:]
                for d in range(1, 4):
                    total += (
                        mask_s[d - 1, here, :]
                        * wx_ref[3 - d : 4 - d, lanes]
                        * pltpu.roll(wide, d, 0)[HALO:]
                    )
                conv = silu(total)
                xc_s[here, lanes] = conv.astype(bf16)
                weight = jnp.dot(ew_s[here, :], pick, preferred_element_type=f32)
                fresh = lax.dot_general(
                    b_s[here, :],
                    (conv * weight).astype(bf16),
                    (((0,), (0,)), ((), ())),
                    preferred_element_type=f32,
                )
                fresh_s[k, :, lanes] = fresh
                keep = jnp.dot(
                    keep_s[k], pick_f, precision=lax.Precision.HIGHEST, preferred_element_type=f32
                )
                state = state * keep[0:1] + fresh
                keep_all = keep_all * keep
            for part in range(size):
                send_s[part, :, lanes] = state[part * slab : (part + 1) * slab].astype(bf16)
            ksend_s[:, lanes] = keep_all[0:1]

        pl.semaphore_wait(barrier, size - 1)
        for distance in range(1, size):
            target = lax.rem(me + distance, size)
            hop(send_s.at[target], recv_s.at[me], distance, send_sem, recv_sem).start()
            hop(ksend_s, krecv_s.at[me], distance, ksend_sem, krecv_sem).start()
        recv_s[me] = send_s[me]
        krecv_s[me] = ksend_s[...]

        @pl.loop(0, tiles)
        def _(tile):
            lanes = pl.ds(pl.multiple_of(tile * LANES, LANES), LANES)
            first_half = lane_iota((CHUNK, LANES)) < head_width
            for k in range(chunks):
                here = pl.ds(k * CHUNK, CHUNK)
                level = l_s[here, :]
                gram = gm_s[k]
                mixes = []
                for j in range(2):
                    head = tile * 2 + j
                    column = pltpu.roll(level, heads_pad - head, 1)[:, 0:1]
                    shift = column - m_s[k, pl.ds(head, 1), :]
                    shift = jnp.minimum(shift, lg_s[k, pl.ds(head, 1), :])
                    mixes.append((jnp.exp2(shift) * gram).astype(bf16))
                conv = xc_s[here, lanes]
                zero = jnp.zeros_like(conv)
                both = jnp.concatenate(
                    [jnp.where(first_half, conv, zero), jnp.where(first_half, zero, conv)], 0
                )
                out = jnp.dot(jnp.concatenate(mixes, 1), both, preferred_element_type=f32)
                y_s[here, lanes] = out + wx_ref[5:6, lanes] * conv.astype(f32)

        for distance in range(1, size):
            source = lax.rem(me - distance + size, size)
            hop(send_s.at[me], recv_s.at[source], distance, send_sem, recv_sem).wait_recv()
            hop(ksend_s, krecv_s.at[source], distance, ksend_sem, krecv_sem).wait_recv()
        run = jnp.zeros((slab, width), f32)
        for part in range(size):
            back_s[part] = run.astype(bf16)
            if part < size - 1:
                run = run * krecv_s[part] + recv_s[part].astype(f32)
        for distance in range(1, size):
            target = lax.rem(me + distance, size)
            hop(back_s.at[target], inc_s.at[me], distance, bsend_sem, brecv_sem).start()
        inc_s[me] = back_s[me]
        for distance in range(1, size):
            source = lax.rem(me - distance + size, size)
            hop(back_s.at[me], inc_s.at[source], distance, bsend_sem, brecv_sem).wait_recv()

        ss_ref[...] = jnp.zeros_like(ss_ref)

        @pl.loop(0, tiles)
        def _(tile):
            lanes = pl.ds(pl.multiple_of(tile * LANES, LANES), LANES)
            pick = selector(tile, 2 * heads_pad, bf16)
            pick_f = selector(tile, heads_pad, f32)
            state = jnp.concatenate(
                [inc_s[part, :, lanes].astype(f32) for part in range(size)], 0
            )
            for k in range(chunks):
                here = pl.ds(k * CHUNK, CHUNK)
                weight = jnp.dot(cw_s[here, :], pick, preferred_element_type=f32)
                carried = jnp.dot(c_s[here, :], state.astype(bf16), preferred_element_type=f32)
                out = y_s[here, lanes] + weight * carried
                gate = zx_ref[pl.ds(k * CHUNK + HALO, CHUNK), lanes].astype(f32)
                out = out * silu(gate)
                ss_ref[here, :] += out * out
                g_ref[here, lanes] = (out * wx_ref[6:7, lanes]).astype(bf16)
                if k < chunks - 1:
                    keep = jnp.dot(
                        keep_s[k],
                        pick_f,
                        precision=lax.Precision.HIGHEST,
                        preferred_element_type=f32,
                    )
                    state = state * keep[0:1] + fresh_s[k, :, lanes]

        for distance in range(1, size):
            target = lax.rem(me + distance, size)
            hop(send_s.at[target], recv_s.at[me], distance, send_sem, recv_sem).wait_send()
            hop(ksend_s, krecv_s.at[me], distance, ksend_sem, krecv_sem).wait_send()
            hop(back_s.at[target], inc_s.at[me], distance, bsend_sem, brecv_sem).wait_send()


def mixer(live, zx, bcdt, idc, idr, wx, wbc, hv):
    size = lax.axis_size("seq")
    rows = zx.shape[0] - HALO
    width = zx.shape[1] // 2
    states = wbc.shape[1] // 2
    heads_pad = hv.shape[1]
    chunks = rows // CHUNK
    slab = states // size
    vmem = pl.BlockSpec(memory_space=pltpu.VMEM)
    dma = pltpu.SemaphoreType.DMA((size - 1,))
    return pl.pallas_call(
        functools.partial(mixer_kernel, live),
        out_shape=(
            jax.ShapeDtypeStruct((rows, width), bf16),
            jax.ShapeDtypeStruct((rows, LANES), f32),
        ),
        in_specs=[vmem] * 7,
        out_specs=(vmem, vmem),
        scratch_shapes=[
            pltpu.VMEM((3, rows, LANES), f32),
            pltpu.VMEM((rows, heads_pad), f32),
            pltpu.VMEM((chunks, heads_pad, CHUNK), f32),
            pltpu.VMEM((chunks, heads_pad, CHUNK), f32),
            pltpu.VMEM((rows, 2 * heads_pad), bf16),
            pltpu.VMEM((rows, 2 * heads_pad), bf16),
            pltpu.VMEM((chunks, 8, heads_pad), f32),
            pltpu.VMEM((rows, states), bf16),
            pltpu.VMEM((rows, states), bf16),
            pltpu.VMEM((chunks, CHUNK, CHUNK), f32),
            pltpu.VMEM((rows, width), bf16),
            pltpu.VMEM((chunks, states, width), f32),
            pltpu.VMEM((rows, width), f32),
            pltpu.VMEM((size, slab, width), bf16),
            pltpu.VMEM((size, slab, width), bf16),
            pltpu.VMEM((1, width), f32),
            pltpu.VMEM((size, 1, width), f32),
            pltpu.VMEM((size, slab, width), bf16),
            pltpu.VMEM((size, slab, width), bf16),
            dma,
            dma,
            dma,
            dma,
            dma,
            dma,
        ],
        compiler_params=pltpu.CompilerParams(
            collective_id=live, has_side_effects=True, vmem_limit_bytes=56 * 1024 * 1024
        ),
        name=f"mixer_{live}",
    )(zx, bcdt, idc, idr, wx, wbc, hv)


def rms_rows(hidden_f, norm_scale):
    return (
        hidden_f
        * lax.rsqrt(jnp.mean(hidden_f * hidden_f, axis=1, keepdims=True) + epsilon)
        * norm_scale[None, :]
    ).astype(bf16)


def local(
    hidden_in,
    doc_ids,
    norm_gain,
    in_zx,
    in_bc,
    in_dt,
    conv_x,
    conv_bc,
    bias_x,
    bias_bc,
    dt_bias,
    a_log,
    d_skip,
    gated_gain,
    out_w,
):
    sections = lax.axis_size("pipe")
    section_index = lax.axis_index("pipe")
    local_width = gated_gain.shape[1]
    full_width = local_width * lax.axis_size("tp")
    heads = dt_bias.shape[1]
    head_width = local_width // heads
    heads_pad = -(-heads // LANES) * LANES
    weight_zx = in_zx[0].reshape(in_zx.shape[1], 2 * local_width)
    weight_small = jnp.concatenate(
        [in_bc[0], jnp.pad(in_dt[0], ((0, 0), (0, heads_pad - heads)))], 1
    )
    wx = jnp.concatenate(
        [
            conv_x[0],
            bias_x,
            jnp.repeat(d_skip, head_width, axis=1),
            gated_gain,
            jnp.zeros_like(gated_gain),
        ],
        0,
    )
    wbc = jnp.concatenate([conv_bc[0], bias_bc, jnp.zeros((3, bias_bc.shape[1]), f32)], 0)
    hv = jnp.pad(
        jnp.concatenate([dt_bias, -jnp.exp(a_log) * LOG2E], 0),
        ((0, 6), (0, heads_pad - heads)),
    )
    row_ids = doc_ids[0].astype(f32)
    edge = lax.ppermute(
        row_ids[-HALO:] + 1.0,
        "seq",
        [(i, i + 1) for i in range(lax.axis_size("seq") - 1)],
    )
    ids_ext = jnp.concatenate([edge - 1.0, row_ids])
    idc = jnp.broadcast_to(ids_ext[:, None], (ids_ext.shape[0], LANES))
    idr = jnp.broadcast_to(row_ids[None, :], (8, row_ids.shape[0]))
    current = hidden_in[0]
    finished = current
    for live in range(sections):
        if live > 0:
            received = lax.ppermute(finished, "pipe", [(live - 1, live)])
            current = jnp.where(section_index == live, received, current)
        current_f = current.astype(f32)
        normed = gathered_rows(rms_rows(current_f, norm_gain[0]), "tp", live)
        halo = live_shift(normed[-HALO:], "seq", 1, live)
        normed = jnp.concatenate([halo, normed], 0)
        zx = jnp.dot(normed, weight_zx, preferred_element_type=f32).astype(bf16)
        bcdt = jnp.dot(normed, weight_small, preferred_element_type=f32)
        gated, squares = mixer(live, zx, bcdt, idc, idr, wx, wbc, hv)
        part = jnp.dot(gated, out_w[0], preferred_element_type=f32)
        total, square = scattered_sum(part, jnp.sum(squares, axis=1), "tp", live)
        branch = total * lax.rsqrt(square / full_width + epsilon)[:, None]
        done = (current_f + branch).astype(bf16)
        finished = done if live == 0 else jnp.where(section_index == live, done, finished)
    return finished[None, None]


def solution(mesh):
    placed = (
        P(None, ("seq", "tp"), None),
        P(None, "seq"),
        P("pipe", None),
        P("pipe", None, None, "tp"),
        P("pipe", None, None),
        P("pipe", None, "tp"),
        P("pipe", None, "tp"),
        P("pipe", None, None),
        P("pipe", "tp"),
        P("pipe", None),
        P("pipe", "tp"),
        P("pipe", "tp"),
        P("pipe", "tp"),
        P("pipe", "tp"),
        P("pipe", "tp", None),
    )
    return jax.shard_map(
        local,
        mesh=mesh,
        in_specs=placed,
        out_specs=P("pipe", None, ("seq", "tp"), None),
        check_vma=False,
    )
```

profile of v0, /device:TPU:11, one launch (start us, length us, event | category | flops | bytes accessed | tf_op | source)
XLA Modules:
  0.0 323.7 jit_solution(4046565579139908982)
XLA Ops:
  0.0 1.8 fusion.5
  1.8 0.7 reduce
  2.5 1.6 broadcast.57.clone
  4.2 1.4 constant_dynamic-update-slice_fusion.3
  5.6 1.7 collective-permute-start
  7.4 0.6 fusion.20
  7.9 3.2 collective-permute-start.2
  11.2 18.2 %copy.18 = bf16[320,8,2,2560]{3,1,2,0:T(8,128)(2,1)} copy(bf16[320,8,2,2560]{3,2,1,0:T(2,128)(2,1)} %bitcast.29) | data formatting | bytes 52428800
  29.4 0.3 copy.17
  29.7 0.7 broadcast_in_dim.32
  30.6 0.7 negate_multiply_fusion
  31.3 1.3 select_maximum_fusion.hv_ref
  32.5 1.3 maximum_maximum_fusion.wbc_ref
  33.9 1.4 concatenate.24.wx_ref
  35.3 0.6 broadcast_add_fusion
  35.9 2.5 constant_dynamic-update-slice_fusion.2
  38.4 0.9 slice.13
  39.3 0.7 collective-permute-start.1
  40.0 21.5 %convolution_convert_fusion.1.zx_ref = bf16[528,5120]{1,0:T(8,128)(2,1)} fusion(bf16[2560,5120]{1,0:T(8,128)(2,1)} %bitcast.30, bf16[512,2560]{1,0:T(8,128)(2,1)} %constant_dynamic-update-slice_fusion.2, bf16[16,2560]{1,0:T(8,128)(2,1)S(1)} %collective-permute-done.1), kind=kOutput, calls=%fused_computation.5 | convolution fusion | flops 13849313280 | bytes 34324480 | tf_op jit(solution)/shard_map/dot_general | solution.py:442
  61.5 4.2 %fusion.15.bcdt_ref = f32[528,384]{1,0:T(8,128)} fusion(bf16[512,2560]{1,0:T(8,128)(2,1)} %constant_dynamic-update-slice_fusion.2, bf16[16,2560]{1,0:T(8,128)(2,1)S(1)} %collective-permute-done.1, bf16[2560,40]{1,0:T(8,128)(2,1)S(1)} %copy.17, bf16[2560,256]{1,0:T(8,128)(2,1)S(1)} %bitcast.38), kind=kOutput, calls=%fused_computation.28 | convolution fusion | flops 1049395200 | bytes 5029888 | tf_op jit(solution)/shard_map/dot_general | solution.py:443
  65.6 0.8 broadcast_in_dim.14.idc_ref
  66.5 0.6 broadcast_in_dim.15.idr_ref
  67.1 4.8 %mixer_0.1 = (bf16[512,2560]{1,0:T(8,128)(2,1)}, f32[512,128]{1,0:T(8,128)}) custom-call(bf16[528,5120]{1,0:T(8,128)(2,1)} %convolution_convert_fusion.1.zx_ref, f32[528,384]{1,0:T(8,128)} %fusion.15.bcdt_ref, f32[528,128]{1,0:T(8,128)} %broadcast_in_dim.14.idc_ref, f32[8,512]{1,0:T(8,128)} %broadcast_in_dim.15.idr_ref, f32[8,2560]{1,0:T(8,128)} %concatenate.24.wx_ref, ...), custom_call_target="tpu_custom_call" | custom-call | tf_op jit(solution)/shard_map/mixer_0/pallas_call | solution.py:330
  71.9 10.8 %fusion.2 = f32[512,2560]{1,0:T(8,128)S(1)} fusion(bf16[512,2560]{1,0:T(8,128)(2,1)} %get-tuple-element.9, bf16[1,2560,2560]{2,1,0:T(8,128)(2,1)} %param.29), kind=kOutput, calls=%fused_computation.2 | convolution fusion | flops 6710886400 | bytes 20971520 | tf_op jit(solution)/shard_map/dot_general | solution.py:445
  82.6 2.4 copy-done.4
  85.1 1.8 collective-permute-start.3
  87.1 0.7 collective-permute-start.4
  87.9 2.8 fusion.8
  90.7 1.3 collective-permute-start.5
  92.0 85.1 %collective-permute-done.5 = bf16[256,2560]{1,0:T(8,128)(2,1)} collective-permute-done((bf16[256,2560]{1,0:T(8,128)(2,1)S(1)}, bf16[256,2560]{1,0:T(8,128)(2,1)}, u32[]{:S(2)}, u32[]{:S(2)}) %collective-permute-start.5) | collective-permute-done | bytes 1310752 | tf_op jit(solution)/shard_map/ppermute | solution.py:436
  177.1 1.9 fusion.9
  179.0 0.2 broadcast.57
  179.2 0.4 constant_dynamic-update-slice_fusion.1
  179.6 2.2 collective-permute-start.6
  181.7 16.2 %collective-permute-done.6 = bf16[256,2560]{1,0:T(8,128)(2,1)S(1)} collective-permute-done((bf16[256,2560]{1,0:T(8,128)(2,1)S(1)}, bf16[256,2560]{1,0:T(8,128)(2,1)S(1)}, u32[]{:S(2)}, u32[]{:S(2)}) %collective-permute-start.6) | collective-permute-done | bytes 1310752 | tf_op jit(solution)/shard_map/ppermute | solution.py:27
  198.1 2.1 collective-permute-start.7
  200.1 3.3 %collective-permute-done.7 = bf16[16,2560]{1,0:T(8,128)(2,1)S(1)} collective-permute-done((bf16[16,2560]{1,0:T(8,128)(2,1)S(1)}, bf16[16,2560]{1,0:T(8,128)(2,1)S(1)}, u32[]{:S(2)}, u32[]{:S(2)}) %collective-permute-start.7) | collective-permute-done | bytes 81952 | tf_op jit(solution)/shard_map/ppermute | solution.py:27
  203.4 20.7 %convolution_convert_fusion.zx_ref = bf16[528,5120]{1,0:T(8,128)(2,1)} fusion(bf16[2560,5120]{1,0:T(8,128)(2,1)} %bitcast.31, bf16[512,2560]{1,0:T(8,128)(2,1)S(1)} %constant_dynamic-update-slice_fusion, bf16[16,2560]{1,0:T(8,128)(2,1)S(1)} %collective-permute-done.7), kind=kOutput, calls=%fused_computation.4 | convolution fusion | flops 13849313280 | bytes 34324480 | tf_op jit(solution)/shard_map/dot_general | solution.py:442
  224.1 2.5 fusion.14.bcdt_ref
  226.5 60.1 %mixer_1.1 = (bf16[512,2560]{1,0:T(8,128)(2,1)}, f32[512,128]{1,0:T(8,128)}) custom-call(bf16[528,5120]{1,0:T(8,128)(2,1)} %convolution_convert_fusion.zx_ref, f32[528,384]{1,0:T(8,128)} %fusion.14.bcdt_ref, f32[528,128]{1,0:T(8,128)} %broadcast_in_dim.14.idc_ref, f32[8,512]{1,0:T(8,128)} %broadcast_in_dim.15.idr_ref, f32[8,2560]{1,0:T(8,128)} %concatenate.24.wx_ref, ...), custom_call_target="tpu_custom_call" | custom-call | tf_op jit(solution)/shard_map/mixer_1/pallas_call | solution.py:330
  286.7 10.7 %fusion = f32[512,2560]{1,0:T(8,128)S(1)} fusion(bf16[512,2560]{1,0:T(8,128)(2,1)} %get-tuple-element.11, bf16[1,2560,2560]{2,1,0:T(8,128)(2,1)} %param.29), kind=kOutput, calls=%fused_computation | convolution fusion | flops 6710886400 | bytes 20971520 | tf_op jit(solution)/shard_map/dot_general | solution.py:445
  297.5 2.3 copy-done.3
  299.8 1.2 dynamic-slice_convert_fusion
  301.0 2.1 collective-permute-start.8
  303.1 0.1 reduce_sum.39
  303.3 3.1 collective-permute-start.9
  306.5 13.1 %collective-permute-done.9 = f32[256]{0:T(256)S(1)} collective-permute-done((f32[256]{0:T(256)S(1)}, f32[256]{0:T(256)S(1)}, u32[]{:S(2)}, u32[]{:S(2)}) %collective-permute-start.9) | collective-permute-done | bytes 1056 | tf_op jit(solution)/shard_map/ppermute | solution.py:27
  319.7 4.0 %fusion.17 = bf16[1,1,256,2560]{3,2,1,0:T(8,128)(2,1)} fusion(bf16[256,2560]{1,0:T(8,128)(2,1)S(1)} %copy-done.2, bf16[256,2560]{1,0:T(8,128)(2,1)} %collective-permute-done.8, f32[512,2560]{1,0:T(8,128)} %copy-done.3, s32[]{:T(128)S(6)} %select_n.29, bf16[256,2560]{1,0:T(8,128)(2,1)S(1)} %get-tuple-element.16, f32[256]{0:T(256)S(1)} %add_rsqrt_fusion, ...), kind=kLoop, calls=%fused_computation.30 | loop fusion | flops 4587520 | bytes 7865349 | tf_op jit(solution)/shard_map/broadcast_in_dim | solution.py:450
  (48 shorter events, 1.1 us)
Async XLA Ops:
  0.0 4.2 %copy-start = (bf16[1,256,2560]{2,1,0:T(8,128)(2,1)S(1)}, bf16[1,256,2560]{2,1,0:T(8,128)(2,1)}, u32[]{:S(2)}) copy-start(bf16[1,256,2560]{2,1,0:T(8,128)(2,1)} %param.15) | copy-start | bytes 3932164
  4.2 3.2 copy-start.11
  5.6 30.3 %collective-permute-start = (bf16[256,2560]{1,0:T(8,128)(2,1)S(1)}, bf16[256,2560]{1,0:T(8,128)(2,1)}, u32[]{:S(2)}, u32[]{:S(2)}) collective-permute-start(bf16[256,2560]{1,0:T(8,128)(2,1)S(1)} %get-tuple-element.18), channel_id=1, source_target_pairs={{0,1},{1,0},{2,3},{3,2},{4,5},{5,4},{6,7},{7,6},{8,9},{9,8},{10,11... | collective-permute-start | bytes 3932168 | tf_op jit(solution)/shard_map/ppermute | solution.py:27
  7.9 27.4 %collective-permute-start.2 = (f32[16]{0:T(128)}, f32[16]{0:T(128)}, u32[]{:S(2)}, u32[]{:S(2)}) collective-permute-start(f32[16]{0:T(128)} %fusion.20), channel_id=1, source_target_pairs={{0,2},{2,4},{4,6},{6,8},{8,10},{10,12},{12,14},{1,3},{3,5},{5,7},{... | collective-permute-start | bytes 200 | tf_op jit(solution)/shard_map/ppermute | solution.py:424
  11.1 18.2 %copy-start.7 = (bf16[1,2560,40]{1,2,0:T(8,128)(2,1)S(1)}, bf16[1,2560,40]{1,2,0:T(8,128)(2,1)}, u32[]{:S(2)}) copy-start(bf16[1,2560,40]{1,2,0:T(8,128)(2,1)} %param.20) | copy-start | bytes 614404
  11.1 21.4 %copy-start.10 = (f32[1,4,256]{2,1,0:T(4,128)S(1)}, f32[1,4,256]{2,1,0:T(4,128)}, u32[]{:S(2)}) copy-start(f32[1,4,256]{2,1,0:T(4,128)} %param.22) | copy-start | bytes 12292
  11.2 22.7 %copy-start.8 = (f32[1,4,2560]{2,1,0:T(4,128)S(1)}, f32[1,4,2560]{2,1,0:T(4,128)}, u32[]{:S(2)}) copy-start(f32[1,4,2560]{2,1,0:T(4,128)} %param.21) | copy-start | bytes 122884
  11.2 22.7 %copy-start.9 = (f32[1,2560]{1,0:T(1,128)S(1)}, f32[1,2560]{1,0:T(1,128)}, u32[]{:S(2)}) copy-start(f32[1,2560]{1,0:T(1,128)} %param.23) | copy-start | bytes 30724
  39.3 0.7 collective-permute-start.1
  40.0 21.5 %copy-start.12 = (bf16[1,2560,256]{2,1,0:T(8,128)(2,1)S(1)}, bf16[1,2560,256]{2,1,0:T(8,128)(2,1)}, u32[]{:S(2)}) copy-start(bf16[1,2560,256]{2,1,0:T(8,128)(2,1)} %param.19) | copy-start | bytes 3932164
  82.6 2.4 copy-start.4
  85.0 1.9 copy-start.6
  85.1 2.8 collective-permute-start.3
  87.1 0.7 collective-permute-start.4
  90.7 1.3 copy-start.1
  90.7 86.4 %collective-permute-start.5 = (bf16[256,2560]{1,0:T(8,128)(2,1)S(1)}, bf16[256,2560]{1,0:T(8,128)(2,1)}, u32[]{:S(2)}, u32[]{:S(2)}) collective-permute-start(bf16[256,2560]{1,0:T(8,128)(2,1)S(1)} %fusion.8), channel_id=1, source_target_pairs={{0,16},{1,17},{2,18},{3,19},{4,20},{5,21},{6,22},{7,23},{8,24},{9,... | collective-permute-start | bytes 3932168 | tf_op jit(solution)/shard_map/ppermute | solution.py:436
  179.6 18.4 %collective-permute-start.6 = (bf16[256,2560]{1,0:T(8,128)(2,1)S(1)}, bf16[256,2560]{1,0:T(8,128)(2,1)S(1)}, u32[]{:S(2)}, u32[]{:S(2)}) collective-permute-start(bf16[256,2560]{1,0:T(8,128)(2,1)S(1)} %get-tuple-element.14), channel_id=1, source_target_pairs={{16,17},{17,16},{18,19},{19,18},{20,21},{21,20},{22,23},{23,22},{2... | collective-permute-start | bytes 3932168 | tf_op jit(solution)/shard_map/ppermute | solution.py:27
  198.1 26.0 %copy-start.13 = (bf16[1,2560,256]{2,1,0:T(8,128)(2,1)S(1)}, bf16[1,2560,256]{2,1,0:T(8,128)(2,1)}, u32[]{:S(2)}) copy-start(bf16[1,2560,256]{2,1,0:T(8,128)(2,1)} %param.19) | copy-start | bytes 3932164
  198.1 5.3 %collective-permute-start.7 = (bf16[16,2560]{1,0:T(8,128)(2,1)S(1)}, bf16[16,2560]{1,0:T(8,128)(2,1)S(1)}, u32[]{:S(2)}, u32[]{:S(2)}) collective-permute-start(bf16[16,2560]{1,0:T(8,128)(2,1)S(1)} %slice.15), channel_id=1, source_target_pairs={{16,18},{18,20},{20,22},{22,24},{24,26},{26,28},{28,30},{17,19},{1... | collective-permute-start | bytes 245768 | tf_op jit(solution)/shard_map/ppermute | solution.py:27
  297.4 2.3 copy-start.3
  299.8 3.3 %copy-start.5 = (f32[512,128]{1,0:T(8,128)S(1)}, f32[512,128]{1,0:T(8,128)}, u32[]{:S(2)}) copy-start(f32[512,128]{1,0:T(8,128)} %get-tuple-element.12) | copy-start | bytes 786436
  299.8 19.9 %copy-start.2 = (bf16[256,2560]{1,0:T(8,128)(2,1)S(1)}, bf16[256,2560]{1,0:T(8,128)(2,1)}, u32[]{:S(2)}) copy-start(bf16[256,2560]{1,0:T(8,128)(2,1)} %copy-done.1) | copy-start | bytes 3932164
  301.0 18.7 %collective-permute-start.8 = (bf16[256,2560]{1,0:T(8,128)(2,1)}, bf16[256,2560]{1,0:T(8,128)(2,1)}, u32[]{:S(2)}, u32[]{:S(2)}) collective-permute-start(bf16[256,2560]{1,0:T(8,128)(2,1)} %dynamic-slice_convert_fusion), channel_id=1, source_target_pairs={{16,17},{17,16},{18,19},{19,18},{20,21},{21,20},{22,23},{23,22},{2... | collective-permute-start | bytes 3932168 | tf_op jit(solution)/shard_map/ppermute | solution.py:27
  303.3 16.3 %collective-permute-start.9 = (f32[256]{0:T(256)S(1)}, f32[256]{0:T(256)S(1)}, u32[]{:S(2)}, u32[]{:S(2)}) collective-permute-start(f32[256]{0:T(256)S(1)} %dynamic_slice.31), channel_id=1, source_target_pairs={{16,17},{17,16},{18,19},{19,18},{20,21},{21,20},{22,23},{23,22},{2... | collective-permute-start | bytes 3080 | tf_op jit(solution)/shard_map/ppermute | solution.py:27
where the time goes:
time: 324 us
  waiting for transfers between devices  118 us (36%)
  matrix products  70.3 us (22%)
  Pallas kernels  64.9 us (20%)
  local copies, waits for them, and re-layouts  33.8 us (10%)
  starting transfers between devices  18.7 us (6%)
  other arithmetic  18 us (6%)
    ppermute x1, waiting for transfers between devices, local(): received = lax.ppermute(finished, 'pipe', [(live - 1, live)])  85.1 us
    pallas_call x2, Pallas kernels, mixer(): pl.pallas_call(functools.partial(mixer_kernel, live), out_shape=(jax.Shap...  64.9 us
    dot_general x2, matrix products, local(): zx = jnp.dot(normed, weight_zx, preferred_element_type=f32).astype(bf16)  42.1 us
    ppermute x8, waiting for transfers between devices, live_shift(): return lax.ppermute(block, ('pipe', axis), route)  32.6 us
    unnamed x30, local copies, waits for them, and re-layouts  23.3 us
    dot_general x2, matrix products, local(): part = jnp.dot(gated, out_w[0], preferred_element_type=f32)  21.5 us
    ppermute x8, starting transfers between devices, live_shift(): return lax.ppermute(block, ('pipe', axis), route)  14.3 us
    dot_general x2, matrix products, local(): bcdt = jnp.dot(normed, weight_small, preferred_element_type=f32)  6.65 us
  transfers between devices with their start and end apart: 10, of which 4 were waited for; matrix products, arithmetic and copies ran while one was open for 8% of the time, Pallas kernels for 0%

commit v1 on v0

--- a/solution.py
+++ b/solution.py
@@ -17,47 +17,13 @@
 bf16 = jnp.bfloat16
 
 
-def live_shift(block, axis, distance, live, wrap=False):
-    size = lax.axis_size(axis)
-    route = []
-    for i in range(size):
-        j = i + distance
-        if wrap or j < size:
-            route.append((live * size + i, live * size + j % size))
-    return lax.ppermute(block, ("pipe", axis), route)
-
-
-def gathered_rows(rows, axis, live):
-    size = lax.axis_size(axis)
-    place = lax.axis_index(axis)
-    count = rows.shape[0]
-    whole = jnp.zeros((size * count,) + rows.shape[1:], rows.dtype)
-    whole = lax.dynamic_update_slice_in_dim(whole, rows, place * count, 0)
-    for step in range(1, size):
-        other = live_shift(rows, axis, step, live, True)
-        source = lax.rem(place - step + size, size)
-        whole = lax.dynamic_update_slice_in_dim(whole, other, source * count, 0)
-    return whole
-
-
-def scattered_sum(rows, squares, axis, live):
-    size = lax.axis_size(axis)
-    place = lax.axis_index(axis)
-    count = rows.shape[0] // size
-    total = lax.dynamic_slice_in_dim(rows, place * count, count, 0)
-    square = lax.dynamic_slice_in_dim(squares, place * count, count, 0)
-    for step in range(1, size):
-        target = lax.rem(place + step, size)
-        piece = lax.dynamic_slice_in_dim(rows, target * count, count, 0).astype(bf16)
-        term = lax.dynamic_slice_in_dim(squares, target * count, count, 0)
-        total = total + live_shift(piece, axis, step, live, True).astype(f32)
-        square = square + live_shift(term, axis, step, live, True)
-    return total, square
-
-
 def silu(value):
     half = 0.5 * value
     return half + half * jnp.tanh(half)
+
+
+def widen(value, count):
+    return jnp.concatenate([value] * count, 1)
 
 
 def split_pair(value):
@@ -84,6 +50,7 @@
     ew_s,
     cw_s,
     keep_s,
+    keepx_s,
     b_s,
     c_s,
     gm_s,
@@ -113,6 +80,8 @@
     slab = states // size
     heads_pad = hv_ref.shape[1]
     head_width = LANES // 2
+    group = 2 if tiles % 2 == 0 else 1
+    span = group * LANES
 
     def lane_iota(shape):
         return lax.broadcasted_iota(jnp.int32, shape, 1)
@@ -121,7 +90,7 @@
         return lax.broadcasted_iota(jnp.int32, shape, 0)
 
     def selector(tile, count, dtype):
-        shape = (count, LANES)
+        shape = (count, span)
         hit = lax.rem(row_iota(shape), heads_pad) == tile * 2 + lane_iota(shape) // head_width
         return hit.astype(f32).astype(dtype)
 
@@ -149,6 +118,7 @@
         square_shape = (CHUNK, CHUNK)
         lower = row_iota(square_shape) >= lane_iota(square_shape)
         lower_f = lower.astype(f32)
+        keep_s[...] = jnp.zeros_like(keep_s)
 
         @pl.loop(0, chunks)
         def _(k):
@@ -178,7 +148,7 @@
                 jnp.exp2(end - level) * step * (seg == last).astype(f32)
             )
             cw_s[here, :] = split_pair(jnp.exp2(level) * (seg == prev).astype(f32))
-            keep_s[k] = jnp.broadcast_to(jnp.exp2(end) * (last == prev).astype(f32), (8, heads_pad))
+            keep_s[pl.ds(k, 1), :] = jnp.exp2(end) * (last == prev).astype(f32)
             for half in range(2):
                 cols = pl.ds(half * states, states)
                 wide = bcdt_ref[pl.ds(base, CHUNK + HALO), cols]
@@ -197,21 +167,23 @@
             same_doc = seg == idr_ref[0:1, pl.ds(base, CHUNK)]
             gm_s[k] = jnp.where(lower & same_doc, gram, 0.0)
 
-        @pl.loop(0, tiles)
-        def _(tile):
-            lanes = pl.ds(pl.multiple_of(tile * LANES, LANES), LANES)
-            x_lanes = pl.ds(pl.multiple_of(width + tile * LANES, LANES), LANES)
+        @pl.loop(0, tiles // group)
+        def _(turn):
+            tile = turn * group
+            lanes = pl.ds(pl.multiple_of(turn * span, span), span)
+            x_lanes = pl.ds(pl.multiple_of(width + turn * span, span), span)
             pick = selector(tile, 2 * heads_pad, bf16)
-            pick_f = selector(tile, heads_pad, f32)
-            state = jnp.zeros((states, LANES), f32)
-            keep_all = jnp.ones((8, LANES), f32)
+            keeps = jnp.dot(split_pair(keep_s[...]), pick, preferred_element_type=f32)
+            keepx_s[:, lanes] = keeps
+            state = jnp.zeros((states, span), f32)
+            keep_all = jnp.ones((1, span), f32)
             for k in range(chunks):
                 here = pl.ds(k * CHUNK, CHUNK)
                 wide = zx_ref[pl.ds(k * CHUNK, CHUNK + HALO), x_lanes].astype(f32)
                 total = wx_ref[4:5, lanes] + wx_ref[3:4, lanes] * wide[HALO:]
                 for d in range(1, 4):
                     total += (
-                        mask_s[d - 1, here, :]
+                        widen(mask_s[d - 1, here, :], group)
                         * wx_ref[3 - d : 4 - d, lanes]
                         * pltpu.roll(wide, d, 0)[HALO:]
                     )
@@ -225,14 +197,12 @@
                     preferred_element_type=f32,
                 )
                 fresh_s[k, :, lanes] = fresh
-                keep = jnp.dot(
-                    keep_s[k], pick_f, precision=lax.Precision.HIGHEST, preferred_element_type=f32
-                )
-                state = state * keep[0:1] + fresh
+                keep = keeps[k : k + 1]
+                state = state * keep + fresh
                 keep_all = keep_all * keep
             for part in range(size):
                 send_s[part, :, lanes] = state[part * slab : (part + 1) * slab].astype(bf16)
-            ksend_s[:, lanes] = keep_all[0:1]
+            ksend_s[:, lanes] = keep_all
 
         pl.semaphore_wait(barrier, size - 1)
         for distance in range(1, size):
@@ -242,28 +212,30 @@
         recv_s[me] = send_s[me]
         krecv_s[me] = ksend_s[...]
 
-        @pl.loop(0, tiles)
-        def _(tile):
-            lanes = pl.ds(pl.multiple_of(tile * LANES, LANES), LANES)
+        @pl.loop(0, tiles // group)
+        def _(turn):
             first_half = lane_iota((CHUNK, LANES)) < head_width
             for k in range(chunks):
                 here = pl.ds(k * CHUNK, CHUNK)
-                level = l_s[here, :]
+                base = turn * group * 2
+                level = pltpu.roll(l_s[here, :], heads_pad - base, 1)
                 gram = gm_s[k]
-                mixes = []
-                for j in range(2):
-                    head = tile * 2 + j
-                    column = pltpu.roll(level, heads_pad - head, 1)[:, 0:1]
-                    shift = column - m_s[k, pl.ds(head, 1), :]
-                    shift = jnp.minimum(shift, lg_s[k, pl.ds(head, 1), :])
-                    mixes.append((jnp.exp2(shift) * gram).astype(bf16))
-                conv = xc_s[here, lanes]
-                zero = jnp.zeros_like(conv)
-                both = jnp.concatenate(
-                    [jnp.where(first_half, conv, zero), jnp.where(first_half, zero, conv)], 0
-                )
-                out = jnp.dot(jnp.concatenate(mixes, 1), both, preferred_element_type=f32)
-                y_s[here, lanes] = out + wx_ref[5:6, lanes] * conv.astype(f32)
+                for i in range(group):
+                    lanes = pl.ds(pl.multiple_of(turn * span + i * LANES, LANES), LANES)
+                    mixes = []
+                    for j in range(2 * i, 2 * i + 2):
+                        shift = level[:, j : j + 1] - m_s[k, pl.ds(base + j, 1), :]
+                        shift = jnp.minimum(shift, lg_s[k, pl.ds(base + j, 1), :])
+                        mixes.append((jnp.exp2(shift) * gram).astype(bf16))
+                    conv = xc_s[here, lanes]
+                    zero = jnp.zeros_like(conv)
+                    both = jnp.concatenate(
+                        [jnp.where(first_half, conv, zero), jnp.where(first_half, zero, conv)], 0
+                    )
+                    out = jnp.dot(
+                        jnp.concatenate(mixes, 1), both, preferred_element_type=f32
+                    )
+                    y_s[here, lanes] = out + wx_ref[5:6, lanes] * conv.astype(f32)
 
         for distance in range(1, size):
             source = lax.rem(me - distance + size, size)
@@ -284,11 +256,11 @@
 
         ss_ref[...] = jnp.zeros_like(ss_ref)
 
-        @pl.loop(0, tiles)
-        def _(tile):
-            lanes = pl.ds(pl.multiple_of(tile * LANES, LANES), LANES)
-            pick = selector(tile, 2 * heads_pad, bf16)
-            pick_f = selector(tile, heads_pad, f32)
+        @pl.loop(0, tiles // group)
+        def _(turn):
+            lanes = pl.ds(pl.multiple_of(turn * span, span), span)
+            pick = selector(turn * group, 2 * heads_pad, bf16)
+            keeps = keepx_s[:, lanes]
             state = jnp.concatenate(
                 [inc_s[part, :, lanes].astype(f32) for part in range(size)], 0
             )
@@ -299,16 +271,14 @@
                 out = y_s[here, lanes] + weight * carried
                 gate = zx_ref[pl.ds(k * CHUNK + HALO, CHUNK), lanes].astype(f32)
                 out = out * silu(gate)
-                ss_ref[here, :] += out * out
+                square = out * out
+                sums = square[:, :LANES]
+                for i in range(1, group):
+                    sums += square[:, i * LANES : (i + 1) * LANES]
+                ss_ref[here, :] += sums
                 g_ref[here, lanes] = (out * wx_ref[6:7, lanes]).astype(bf16)
                 if k < chunks - 1:
-                    keep = jnp.dot(
-                        keep_s[k],
-                        pick_f,
-                        precision=lax.Precision.HIGHEST,
-                        preferred_element_type=f32,
-                    )
-                    state = state * keep[0:1] + fresh_s[k, :, lanes]
+                    state = state * keeps[k : k + 1] + fresh_s[k, :, lanes]
 
         for distance in range(1, size):
             target = lax.rem(me + distance, size)
@@ -342,7 +312,8 @@
             pltpu.VMEM((chunks, heads_pad, CHUNK), f32),
             pltpu.VMEM((rows, 2 * heads_pad), bf16),
             pltpu.VMEM((rows, 2 * heads_pad), bf16),
-            pltpu.VMEM((chunks, 8, heads_pad), f32),
+            pltpu.VMEM((8, heads_pad), f32),
+            pltpu.VMEM((8, width), f32),
             pltpu.VMEM((rows, states), bf16),
             pltpu.VMEM((rows, states), bf16),
             pltpu.VMEM((chunks, CHUNK, CHUNK), f32),
@@ -369,12 +340,356 @@
     )(zx, bcdt, idc, idr, wx, wbc, hv)
 
 
-def rms_rows(hidden_f, norm_scale):
-    return (
-        hidden_f
-        * lax.rsqrt(jnp.mean(hidden_f * hidden_f, axis=1, keepdims=True) + epsilon)
-        * norm_scale[None, :]
-    ).astype(bf16)
+def piece_width(features):
+    return max(w for w in (512, 256, 128) if features % w == 0)
+
+
+def boundary_kernel(out_live, in_live, *refs):
+    refs = iter(refs)
+    take = lambda count: [next(refs) for _ in range(count)]
+    sends_rows = out_live is None
+    if out_live is not None:
+        gated_ref, squares_ref, weight_out = take(3)
+    (hidden_ref,) = take(1)
+    if in_live is not None:
+        gain_ref, weight_zx, weight_small = take(3)
+    if out_live is not None:
+        (done_ref,) = take(1)
+    if in_live is not None:
+        zx_ref, small_ref = take(2)
+    if out_live is not None:
+        wo_s, part_s, psend_s, precv_s, sqsend_s, sqrecv_s = take(6)
+        wo_sem, psend_sem, precv_sem, sqsend_sem, sqrecv_sem = take(5)
+    if in_live is not None:
+        rows_s, wz_s, acc_s, accb_s, squares_s, gain_s = take(6)
+        wz_sem, rsend_sem, rrecv_sem, hsend_sem, hrecv_sem = take(5)
+
+    tp = lax.axis_size("tp")
+    shards = lax.axis_size("seq")
+    t = lax.axis_index("tp")
+    s = lax.axis_index("seq")
+    pipe = lax.axis_index("pipe")
+    count, features = hidden_ref.shape
+    piece = piece_width(features)
+    pieces = features // piece
+    has_next = (t == tp - 1) & (s < shards - 1)
+    from_live = in_live if sends_rows else out_live
+
+    def peer(distance):
+        return lax.rem(t + distance, tp)
+
+    def cols(c):
+        return pl.ds(c * piece, piece)
+
+    def row_copy(source, c, distance):
+        return pltpu.make_async_remote_copy(
+            src_ref=source.at[:, cols(c)],
+            dst_ref=rows_s.at[c, pl.ds(pl.multiple_of(HALO + t * count, HALO), count), :],
+            send_sem=rsend_sem.at[c, distance],
+            recv_sem=rrecv_sem.at[c, distance],
+            device_id={"pipe": in_live, "tp": peer(distance)},
+            device_id_type=MESH,
+        )
+
+    def row_arrival(c, distance):
+        start = HALO + lax.rem(t - distance + tp, tp) * count
+        return pltpu.make_async_remote_copy(
+            src_ref=rows_s.at[c, pl.ds(0, count), :],
+            dst_ref=rows_s.at[c, pl.ds(pl.multiple_of(start, HALO), count), :],
+            send_sem=rsend_sem.at[c, distance],
+            recv_sem=rrecv_sem.at[c, distance],
+            device_id={"pipe": in_live, "tp": peer(distance)},
+            device_id_type=MESH,
+        )
+
+    def halo_copy(source, c, target):
+        return pltpu.make_async_remote_copy(
+            src_ref=source.at[pl.ds(count - HALO, HALO), cols(c)],
+            dst_ref=rows_s.at[c, pl.ds(0, HALO), :],
+            send_sem=hsend_sem.at[c, target],
+            recv_sem=hrecv_sem.at[c],
+            device_id={"pipe": in_live, "seq": s + 1, "tp": target},
+            device_id_type=MESH,
+        )
+
+    def part_copy(c, distance):
+        return pltpu.make_async_remote_copy(
+            src_ref=psend_s.at[c, peer(distance)],
+            dst_ref=precv_s.at[c, distance - 1],
+            send_sem=psend_sem.at[c, distance - 1],
+            recv_sem=precv_sem.at[c, distance - 1],
+            device_id={"tp": peer(distance)},
+            device_id_type=MESH,
+        )
+
+    def square_copy(distance):
+        return pltpu.make_async_remote_copy(
+            src_ref=sqsend_s.at[peer(distance)],
+            dst_ref=sqrecv_s.at[distance - 1],
+            send_sem=sqsend_sem.at[distance - 1],
+            recv_sem=sqrecv_sem.at[distance - 1],
+            device_id={"tp": peer(distance)},
+            device_id_type=MESH,
+        )
+
+    def greet(**where):
+        pl.semaphore_signal(
+            pltpu.get_barrier_semaphore(), inc=1, device_id=where, device_id_type=MESH
+        )
+
+    def meet(number, with_next):
+        barrier = pltpu.get_barrier_semaphore()
+        if not with_next:
+            if number:
+                pl.semaphore_wait(barrier, number)
+            return
+
+        @pl.when(has_next)
+        def _():
+            pl.semaphore_wait(barrier, number + tp)
+
+        if number:
+
+            @pl.when(jnp.logical_not(has_next))
+            def _():
+                pl.semaphore_wait(barrier, number)
+
+    def weight_copy(c):
+        return pltpu.make_async_copy(
+            weight_zx.at[pl.ds(c * piece, piece)], wz_s.at[c % 2], wz_sem.at[c % 2]
+        )
+
+    def forward_rows(source, c):
+        first = 1 if sends_rows else 0
+        for distance in range(first, tp):
+            row_copy(source, c, distance).start()
+
+        @pl.when(has_next)
+        def _():
+            for target in range(tp):
+                halo_copy(source, c, target).start()
+
+    def drain_rows(source):
+        for c in range(pieces):
+            for distance in range(1 if sends_rows else 0, tp):
+                row_copy(source, c, distance).wait_send()
+
+        @pl.when(has_next)
+        def _():
+            for c in range(pieces):
+                for target in range(tp):
+                    halo_copy(source, c, target).wait_send()
+
+    def project():
+        for c in range(min(2, pieces)):
+            weight_copy(c).start()
+        for distance in range(1 if sends_rows else 0, tp):
+            greet(pipe=from_live, tp=lax.rem(t - distance + tp, tp))
+
+        @pl.when(s > 0)
+        def _():
+            greet(pipe=from_live, seq=s - 1, tp=tp - 1)
+
+        if sends_rows:
+            meet(tp - 1, True)
+            for c in range(pieces):
+                forward_rows(hidden_ref, c)
+            for c in range(pieces):
+                mine = pl.ds(pl.multiple_of(HALO + t * count, HALO), count)
+                rows_s[c, mine, :] = hidden_ref[:, cols(c)]
+
+        @pl.when(s == 0)
+        def _():
+            rows_s[:, pl.ds(0, HALO), :] = jnp.zeros((pieces, HALO, piece), bf16)
+
+        total_rows = rows_s.shape[1]
+        out_cols = zx_ref.shape[1]
+        tile = piece_width(out_cols)
+        squares_s[...] = jnp.zeros_like(squares_s)
+        for c in range(pieces):
+            for distance in range(1 if sends_rows else 0, tp):
+                row_arrival(c, distance).wait_recv()
+
+            @pl.when(s > 0)
+            def _():
+                halo_copy(hidden_ref, c, 0).wait_recv()
+
+            weight_copy(c).wait()
+            values = rows_s[c].astype(f32)
+            square = values * values
+            sums = square[:, :LANES]
+            for i in range(1, piece // LANES):
+                sums += square[:, i * LANES : (i + 1) * LANES]
+            squares_s[...] += sums
+            gain_s[...] = (values * gain_ref[0:1, cols(c)]).astype(bf16)
+            last = c == pieces - 1
+            if last:
+                mean = jnp.sum(squares_s[...], axis=1, keepdims=True) / features
+                squares_s[...] = jnp.broadcast_to(
+                    lax.rsqrt(mean + epsilon), (total_rows, LANES)
+                )
+            small = jnp.dot(
+                gain_s[...], weight_small[pl.ds(c * piece, piece), :], preferred_element_type=f32
+            )
+            if c > 0:
+                small += accb_s[...]
+            if last:
+                small_ref[...] = small * squares_s[:, 0:1]
+            else:
+                accb_s[...] = small
+
+            @pl.loop(0, out_cols // tile)
+            def _(n):
+                at = pl.ds(pl.multiple_of(n * tile, tile), tile)
+                value = jnp.dot(
+                    gain_s[...], wz_s[c % 2, :, at], preferred_element_type=f32
+                )
+                if c > 0:
+                    value += acc_s[:, at]
+                if last:
+                    zx_ref[:, at] = (value * widen(squares_s[...], tile // LANES)).astype(bf16)
+                else:
+                    acc_s[:, at] = value
+
+            if c + 2 < pieces:
+                weight_copy(c + 2).start()
+        if sends_rows:
+            drain_rows(hidden_ref)
+
+    def finish():
+        for c in range(pieces):
+            pltpu.make_async_copy(weight_out.at[:, cols(c)], wo_s.at[c], wo_sem.at[c]).start()
+        for distance in range(1, tp):
+            greet(tp=peer(distance))
+        for target in range(tp):
+            own = squares_ref[target * count : (target + 1) * count, :]
+            sqsend_s[target] = lax.dot_general(
+                jnp.ones((8, LANES), f32),
+                own,
+                (((1,), (1,)), ((), ())),
+                precision=lax.Precision.HIGHEST,
+                preferred_element_type=f32,
+            )
+        for c in range(pieces):
+            pltpu.make_async_copy(weight_out.at[:, cols(c)], wo_s.at[c], wo_sem.at[c]).wait()
+            for target in range(tp):
+                value = jnp.dot(
+                    gated_ref[target * count : (target + 1) * count, :],
+                    wo_s[c],
+                    preferred_element_type=f32,
+                )
+                part_s[c, target] = value
+                psend_s[c, target] = value.astype(bf16)
+            if c == 0:
+                meet(tp - 1 if in_live is None else 2 * tp - 1, in_live is not None)
+                for distance in range(1, tp):
+                    square_copy(distance).start()
+            for distance in range(1, tp):
+                part_copy(c, distance).start()
+        sums = sqsend_s[t]
+        for distance in range(1, tp):
+            square_copy(distance).wait_recv()
+            sums += sqrecv_s[distance - 1]
+        sums = lax.dot_general(
+            sums,
+            jnp.full((8, LANES), 0.125, f32),
+            (((0,), (0,)), ((), ())),
+            precision=lax.Precision.HIGHEST,
+            preferred_element_type=f32,
+        )
+        scale = lax.rsqrt(sums / (gated_ref.shape[1] * tp) + epsilon)
+        for c in range(pieces):
+            total = part_s[c, t]
+            for distance in range(1, tp):
+                part_copy(c, distance).wait_recv()
+                total += precv_s[c, distance - 1].astype(f32)
+            done_ref[:, cols(c)] = (
+                hidden_ref[:, cols(c)].astype(f32) + total * widen(scale, piece // LANES)
+            ).astype(bf16)
+            if in_live is not None:
+                forward_rows(done_ref, c)
+        for distance in range(1, tp):
+            square_copy(distance).wait_send()
+            for c in range(pieces):
+                part_copy(c, distance).wait_send()
+        if in_live is not None:
+            drain_rows(done_ref)
+
+    if out_live is not None:
+        pl.when(pipe == out_live)(finish)
+    if in_live is not None:
+        pl.when(pipe == in_live)(project)
+
+
+def boundary(out_live, in_live, out_args, hidden, in_args):
+    tp = lax.axis_size("tp")
+    count, features = hidden.shape
+    piece = piece_width(features)
+    pieces = features // piece
+    vmem = pl.BlockSpec(memory_space=pltpu.VMEM)
+    hbm = pl.BlockSpec(memory_space=pl.ANY)
+    dma = pltpu.SemaphoreType.DMA
+    args, specs, outs, scratch = [], [], [], []
+    peers = max(1, tp - 1)
+    if out_live is not None:
+        args += out_args
+        specs += [vmem, vmem, hbm]
+    args.append(hidden)
+    specs.append(vmem)
+    if in_live is not None:
+        args += in_args
+        specs += [vmem, hbm, vmem]
+    if out_live is not None:
+        outs.append(jax.ShapeDtypeStruct((count, features), bf16))
+        width = out_args[2].shape[0]
+        scratch += [
+            pltpu.VMEM((pieces, width, piece), bf16),
+            pltpu.VMEM((pieces, tp, count, piece), f32),
+            pltpu.VMEM((pieces, tp, count, piece), bf16),
+            pltpu.VMEM((pieces, peers, count, piece), bf16),
+            pltpu.VMEM((tp, 8, count), f32),
+            pltpu.VMEM((peers, 8, count), f32),
+            dma((pieces,)),
+            dma((pieces, peers)),
+            dma((pieces, peers)),
+            dma((peers,)),
+            dma((peers,)),
+        ]
+    if in_live is not None:
+        rows = HALO + tp * count
+        wide, small = in_args[1].shape[1], in_args[2].shape[1]
+        outs += [
+            jax.ShapeDtypeStruct((rows, wide), bf16),
+            jax.ShapeDtypeStruct((rows, small), f32),
+        ]
+        scratch += [
+            pltpu.VMEM((pieces, rows, piece), bf16),
+            pltpu.VMEM((2, piece, wide), bf16),
+            pltpu.VMEM((rows, wide), f32),
+            pltpu.VMEM((rows, small), f32),
+            pltpu.VMEM((rows, LANES), f32),
+            pltpu.VMEM((rows, piece), bf16),
+            dma((2,)),
+            dma((pieces, tp)),
+            dma((pieces, tp)),
+            dma((pieces, tp)),
+            dma((pieces,)),
+        ]
+    sections = lax.axis_size("pipe")
+    step = 0 if out_live is None else out_live + 1
+    return pl.pallas_call(
+        functools.partial(boundary_kernel, out_live, in_live),
+        out_shape=tuple(outs),
+        in_specs=specs,
+        out_specs=tuple([vmem] * len(outs)),
+        scratch_shapes=scratch,
+        compiler_params=pltpu.CompilerParams(
+            collective_id=sections + step,
+            has_side_effects=True,
+            vmem_limit_bytes=63 * 1024 * 1024,
+        ),
+        name=f"boundary_{step}",
+    )(*args)
 
 
 def local(
@@ -397,7 +712,6 @@
     sections = lax.axis_size("pipe")
     section_index = lax.axis_index("pipe")
     local_width = gated_gain.shape[1]
-    full_width = local_width * lax.axis_size("tp")
     heads = dt_bias.shape[1]
     head_width = local_width // heads
     heads_pad = -(-heads // LANES) * LANES
@@ -429,23 +743,19 @@
     ids_ext = jnp.concatenate([edge - 1.0, row_ids])
     idc = jnp.broadcast_to(ids_ext[:, None], (ids_ext.shape[0], LANES))
     idr = jnp.broadcast_to(row_ids[None, :], (8, row_ids.shape[0]))
+    gain = jnp.broadcast_to(norm_gain, (8, norm_gain.shape[1]))
+    in_args = [gain, weight_zx, weight_small]
+    zx, bcdt = boundary(None, 0, None, hidden_in[0], in_args)
     current = hidden_in[0]
-    finished = current
+    finished = None
     for live in range(sections):
-        if live > 0:
-            received = lax.ppermute(finished, "pipe", [(live - 1, live)])
-            current = jnp.where(section_index == live, received, current)
-        current_f = current.astype(f32)
-        normed = gathered_rows(rms_rows(current_f, norm_gain[0]), "tp", live)
-        halo = live_shift(normed[-HALO:], "seq", 1, live)
-        normed = jnp.concatenate([halo, normed], 0)
-        zx = jnp.dot(normed, weight_zx, preferred_element_type=f32).astype(bf16)
-        bcdt = jnp.dot(normed, weight_small, preferred_element_type=f32)
         gated, squares = mixer(live, zx, bcdt, idc, idr, wx, wbc, hv)
-        part = jnp.dot(gated, out_w[0], preferred_element_type=f32)
-        total, square = scattered_sum(part, jnp.sum(squares, axis=1), "tp", live)
-        branch = total * lax.rsqrt(square / full_width + epsilon)[:, None]
-        done = (current_f + branch).astype(bf16)
+        out_args = [gated, squares, out_w[0]]
+        if live + 1 < sections:
+            done, zx, bcdt = boundary(live, live + 1, out_args, current, in_args)
+            current = lax.ppermute(done, "pipe", [(live, live + 1)])
+        else:
+            (done,) = boundary(live, None, out_args, current, None)
         finished = done if live == 0 else jnp.where(section_index == live, done, finished)
     return finished[None, None]
 

time: 324 us -> 220 us (0.68)
  Pallas kernels: 64.9 us -> 187 us
  waiting for transfers between devices: 118 us -> 0.01 us
  matrix products: 70.3 us -> 0 us
  starting transfers between devices: 18.7 us -> 4.46 us
  local copies, waits for them, and re-layouts: 33.8 us -> 21.7 us
  other arithmetic: 18 us -> 6.21 us
    pallas_call x0 -> x3, Pallas kernels: none -> 146 us  [boundary(): pl.pallas_call(functools.partial(boundary_kernel, out_live, in_live), out...]
    ppermute x9 -> x1, waiting for transfers between devices: 118 us -> 0.01 us  [local(): current = lax.ppermute(done, 'pipe', [(live, live + 1)])]
    dot_general x6 -> x0, matrix products: 70.3 us -> none  [the longest x2 42.1 us: local(): zx = jnp.dot(normed, weight_zx, preferred_element_type=f32).astype(bf16)]
    pallas_call x2, Pallas kernels: 64.9 us -> 40.3 us  [mixer(): pl.pallas_call(functools.partial(mixer_kernel, live), out_shape=(jax.Shap...]
    ppermute x9 -> x1, starting transfers between devices: 15.6 us -> 1.29 us  [local(): current = lax.ppermute(done, 'pipe', [(live, live + 1)])]
    unnamed x30 -> x24, local copies, waits for them, and re-layouts: 23.3 us -> 18.7 us
    reduce_sum x4 -> x0, other arithmetic: 3.93 us -> none  [the longest x2 3.64 us: rms_rows(): jnp.mean(hidden_f * hidden_f, axis=1, keepdims=True) + epsilon]
  transfers between devices with their start and end apart: 10 -> 2, of which waited for: 4 -> 0; matrix products, arithmetic and copies ran while one was open for 8% -> 10% of each run, Pallas kernels for 0% -> 18%
where the time goes in v1:
time: 220 us; the launch traced here: 219 us
  Pallas kernels  187 us (85%)
  local copies, waits for them, and re-layouts  21.7 us (10%)
  other arithmetic  6.21 us (3%)
  starting transfers between devices  4.46 us (2%)
    pallas_call x3, Pallas kernels, boundary(): pl.pallas_call(functools.partial(boundary_kernel, out_live, in_live), out...  146 us
    pallas_call x2, Pallas kernels, mixer(): pl.pallas_call(functools.partial(mixer_kernel, live), out_shape=(jax.Shap...  40.3 us
    unnamed x24, local copies, waits for them, and re-layouts  18.7 us
  transfers between devices with their start and end apart: 2, of which 0 were waited for; matrix products, arithmetic and copies ran while one was open for 10% of the time, Pallas kernels for 18%

profile of v1, /device:TPU:11, one launch (start us, length us, event | category | flops | bytes accessed | tf_op | source)
XLA Modules:
  0.0 219.4 jit_solution(18012361917445152117)
XLA Ops:
  0.0 0.7 convert_element_type.11
  0.7 0.1 fusion.2
  0.8 3.2 %collective-permute-start = (f32[16]{0:T(128)S(1)}, f32[16]{0:T(128)S(1)}, u32[]{:S(2)}, u32[]{:S(2)}) collective-permute-start(f32[16]{0:T(128)S(1)} %fusion.2), channel_id=1, source_target_pairs={{0,2},{2,4},{4,6},{6,8},{8,10},{10,12},{12,14},{1,3},{3,5},{5,7},{... | collective-permute-start | bytes 200 | tf_op jit(solution)/shard_map/ppermute | solution.py:738
  3.9 0.0 copy-start.1
  3.9 0.0 copy-start.9
  4.0 0.0 copy-start.10
  4.0 0.0 copy-start
  4.0 18.3 %copy.17 = bf16[320,8,2,2560]{3,1,2,0:T(8,128)(2,1)} copy(bf16[320,8,2,2560]{3,2,1,0:T(2,128)(2,1)} %bitcast.19) | data formatting | bytes 52428800
  22.2 0.0 copy-done.1
  22.3 0.3 copy.16
  22.6 0.0 copy-done.9
  22.6 0.1 broadcast_in_dim.37
  22.7 0.1 broadcast_in_dim.38
  22.8 0.0 copy-done.10
  22.8 0.0 copy-done
  22.8 0.0 copy-start.5
  22.8 0.0 copy-start.8
  22.8 0.0 copy-start.6
  22.8 0.0 copy-start.7
  22.8 1.5 fusion.1.refs_3_.refs_6_
  24.4 0.0 copy-done.5
  24.4 0.1 pad.14.clone
  24.5 0.0 copy-done.8
  24.5 0.6 select_maximum_fusion.hv_ref
  25.1 0.0 copy-done.6
  25.1 0.0 copy-done.7
  25.1 0.7 maximum_maximum_fusion.wbc_ref
  25.8 0.6 broadcast_in_dim.34.refs_1_.refs_4_
  26.4 0.0 copy-start.2
  26.4 0.0 copy-start.3
  26.4 0.0 copy-start.4
  26.4 5.0 %boundary_0.1 = (bf16[528,5120]{1,0:T(8,128)(2,1)}, f32[528,384]{1,0:T(8,128)}) custom-call(bf16[256,2560]{1,0:T(8,128)(2,1)} %bitcast.20, f32[8,2560]{1,0:T(8,128)} %broadcast_in_dim.34.refs_1_.refs_4_, bf16[2560,5120]{1,0:T(8,128)(2,1)} %bitcast.15, bf16[2560,384]{1,0:T(8,128)(2,1)} %fusion.1.refs_3_.refs_6_), custom_call_target="tpu_custom_call" | custom-call | tf_op jit(solution)/shard_map/boundary_0/pallas_call | solution.py:680
  31.4 0.0 copy-done.2
  31.4 0.0 copy-done.3
  31.4 0.0 copy-done.4
  31.4 0.7 concatenate.17.wx_ref
  32.1 0.0 collective-permute-done
  32.1 0.1 pad_maximum_fusion
  32.2 0.8 broadcast_in_dim.35.idc_ref
  33.1 0.6 broadcast_in_dim.36.idr_ref
  33.7 4.8 %mixer_0.1 = (bf16[512,2560]{1,0:T(8,128)(2,1)}, f32[512,128]{1,0:T(8,128)}) custom-call(bf16[528,5120]{1,0:T(8,128)(2,1)} %get-tuple-element.14.zx_ref, f32[528,384]{1,0:T(8,128)} %get-tuple-element.15.bcdt_ref, f32[528,128]{1,0:T(8,128)} %broadcast_in_dim.35.idc_ref, f32[8,512]{1,0:T(8,128)} %broadcast_in_dim.36.idr_ref, f32[8,2560]{1,0:T(8,128)} %concatenate.17.wx_ref, ...), custom_call_target="tpu_custom_call" | custom-call | tf_op jit(solution)/shard_map/mixer_0/pallas_call | solution.py:300
  38.5 118.3 %boundary_1.1 = (bf16[256,2560]{1,0:T(8,128)(2,1)}, bf16[528,5120]{1,0:T(8,128)(2,1)}, f32[528,384]{1,0:T(8,128)}) custom-call(bf16[512,2560]{1,0:T(8,128)(2,1)} %get-tuple-element.16.refs_0_, f32[512,128]{1,0:T(8,128)} %get-tuple-element.17.refs_1_, bf16[2560,2560]{1,0:T(8,128)(2,1)} %bitcast.17, bf16[256,2560]{1,0:T(8,128)(2,1)} %bitcast.21, ...), custom_call_target="tpu_custom_call" | custom-call | tf_op jit(solution)/shard_map/boundary_1/pallas_call | solution.py:680
  156.8 1.3 collective-permute-start.1
  158.1 35.5 %mixer_1.1 = (bf16[512,2560]{1,0:T(8,128)(2,1)}, f32[512,128]{1,0:T(8,128)}) custom-call(bf16[528,5120]{1,0:T(8,128)(2,1)} %get-tuple-element.18.zx_ref, f32[528,384]{1,0:T(8,128)} %get-tuple-element.19.bcdt_ref, f32[528,128]{1,0:T(8,128)} %broadcast_in_dim.35.idc_ref, f32[8,512]{1,0:T(8,128)} %broadcast_in_dim.36.idr_ref, f32[8,2560]{1,0:T(8,128)} %concatenate.17.wx_ref, ...), custom_call_target="tpu_custom_call" | custom-call | tf_op jit(solution)/shard_map/mixer_1/pallas_call | solution.py:300
  193.7 0.0 collective-permute-done.1.refs_3_
  193.7 23.2 %boundary_2.1 = bf16[256,2560]{1,0:T(8,128)(2,1)} custom-call(bf16[512,2560]{1,0:T(8,128)(2,1)} %get-tuple-element.20.refs_0_, f32[512,128]{1,0:T(8,128)} %get-tuple-element.21.refs_1_, bf16[2560,2560]{1,0:T(8,128)(2,1)} %bitcast.18, bf16[256,2560]{1,0:T(8,128)(2,1)} %collective-permute-done.1.refs_3_), custom_call_target="tpu_custom_call" | custom-call | tf_op jit(solution)/shard_map/boundary_2/pallas_call | solution.py:680
  216.8 2.5 %select_bitcast_fusion = bf16[1,1,256,2560]{3,2,1,0:T(8,128)(2,1)} fusion(bf16[256,2560]{1,0:T(8,128)(2,1)} %boundary_2.1, bf16[256,2560]{1,0:T(8,128)(2,1)} %get-tuple-element.22, pred[]{:T(512)S(6)} %eq.3), kind=kLoop, calls=%fused_computation.3 | loop fusion | flops 655360 | bytes 3932161 | tf_op jit(solution)/shard_map/broadcast_in_dim | solution.py:760
  (5 shorter events, 0.0 us)
Async XLA Ops:
  0.8 31.4 %collective-permute-start = (f32[16]{0:T(128)S(1)}, f32[16]{0:T(128)S(1)}, u32[]{:S(2)}, u32[]{:S(2)}) collective-permute-start(f32[16]{0:T(128)S(1)} %fusion.2), channel_id=1, source_target_pairs={{0,2},{2,4},{4,6},{6,8},{8,10},{10,12},{12,14},{1,3},{3,5},{5,7},{... | collective-permute-start | bytes 200 | tf_op jit(solution)/shard_map/ppermute | solution.py:738
  3.9 18.3 %copy-start.1 = (bf16[1,2560,40]{1,2,0:T(8,128)(2,1)S(1)}, bf16[1,2560,40]{1,2,0:T(8,128)(2,1)}, u32[]{:S(2)}) copy-start(bf16[1,2560,40]{1,2,0:T(8,128)(2,1)} %param.20) | copy-start | bytes 614404
  3.9 18.6 %copy-start.9 = (f32[1,40]{1,0:T(1,128)S(1)}, f32[1,40]{1,0:T(1,128)}, u32[]{:S(2)}) copy-start(f32[1,40]{1,0:T(1,128)} %param.27) | copy-start | bytes 484
  4.0 18.8 %copy-start.10 = (f32[1,40]{1,0:T(1,128)S(1)}, f32[1,40]{1,0:T(1,128)}, u32[]{:S(2)}) copy-start(f32[1,40]{1,0:T(1,128)} %param.26) | copy-start | bytes 484
  4.0 18.8 %copy-start = (bf16[1,2560,256]{2,1,0:T(8,128)(2,1)S(1)}, bf16[1,2560,256]{2,1,0:T(8,128)(2,1)}, u32[]{:S(2)}) copy-start(bf16[1,2560,256]{2,1,0:T(8,128)(2,1)} %param.19) | copy-start | bytes 3932164
  22.8 1.6 copy-start.5
  22.8 1.7 copy-start.8
  22.8 2.3 %copy-start.6 = (f32[1,4,256]{2,1,0:T(4,128)S(1)}, f32[1,4,256]{2,1,0:T(4,128)}, u32[]{:S(2)}) copy-start(f32[1,4,256]{2,1,0:T(4,128)} %param.22) | copy-start | bytes 12292
  22.8 2.3 %copy-start.7 = (f32[1,256]{1,0:T(1,128)S(1)}, f32[1,256]{1,0:T(1,128)}, u32[]{:S(2)}) copy-start(f32[1,256]{1,0:T(1,128)} %param.24) | copy-start | bytes 3076
  26.4 5.0 %copy-start.2 = (f32[1,4,2560]{2,1,0:T(4,128)S(1)}, f32[1,4,2560]{2,1,0:T(4,128)}, u32[]{:S(2)}) copy-start(f32[1,4,2560]{2,1,0:T(4,128)} %param.21) | copy-start | bytes 122884
  26.4 5.0 %copy-start.3 = (f32[1,2560]{1,0:T(1,128)S(1)}, f32[1,2560]{1,0:T(1,128)}, u32[]{:S(2)}) copy-start(f32[1,2560]{1,0:T(1,128)} %param.23) | copy-start | bytes 30724
  26.4 5.0 %copy-start.4 = (f32[1,2560]{1,0:T(1,128)S(1)}, f32[1,2560]{1,0:T(1,128)}, u32[]{:S(2)}) copy-start(f32[1,2560]{1,0:T(1,128)} %param.28) | copy-start | bytes 30724
  156.8 36.8 %collective-permute-start.1 = (bf16[256,2560]{1,0:T(8,128)(2,1)}, bf16[256,2560]{1,0:T(8,128)(2,1)}, u32[]{:S(2)}, u32[]{:S(2)}) collective-permute-start(bf16[256,2560]{1,0:T(8,128)(2,1)} %get-tuple-element.22), channel_id=1, source_target_pairs={{0,16},{1,17},{2,18},{3,19},{4,20},{5,21},{6,22},{7,23},{8,24},{9,... | collective-permute-start | bytes 3932168 | tf_op jit(solution)/shard_map/ppermute | solution.py:756

commit v2 on v1

--- a/solution.py
+++ b/solution.py
@@ -34,8 +34,11 @@
 
 def mixer_kernel(
     live,
-    zx_ref,
+    x_ref,
     bcdt_ref,
+    scaled_ref,
+    scale_ref,
+    weight_zx,
     idc_ref,
     idr_ref,
     wx_ref,
@@ -63,6 +66,11 @@
     krecv_s,
     back_s,
     inc_s,
+    rows_s,
+    wz_s,
+    z_s,
+    rows_sem,
+    wz_sem,
     send_sem,
     recv_sem,
     ksend_sem,
@@ -107,6 +115,17 @@
     @pl.when(lax.axis_index("pipe") == live)
     def _():
         barrier = pltpu.get_barrier_semaphore()
+        rows_copy = pltpu.make_async_copy(scaled_ref.at[pl.ds(HALO, rows)], rows_s, rows_sem)
+        rows_copy.start()
+        gate_tile = wz_s.shape[2]
+
+        def gate_copy(n):
+            return pltpu.make_async_copy(
+                weight_zx.at[:, pl.ds(n * gate_tile, gate_tile)], wz_s.at[n], wz_sem.at[n]
+            )
+
+        for n in range(width // gate_tile):
+            gate_copy(n).start()
         for distance in range(1, size):
             pl.semaphore_signal(
                 barrier,
@@ -171,7 +190,6 @@
         def _(turn):
             tile = turn * group
             lanes = pl.ds(pl.multiple_of(turn * span, span), span)
-            x_lanes = pl.ds(pl.multiple_of(width + turn * span, span), span)
             pick = selector(tile, 2 * heads_pad, bf16)
             keeps = jnp.dot(split_pair(keep_s[...]), pick, preferred_element_type=f32)
             keepx_s[:, lanes] = keeps
@@ -179,7 +197,7 @@
             keep_all = jnp.ones((1, span), f32)
             for k in range(chunks):
                 here = pl.ds(k * CHUNK, CHUNK)
-                wide = zx_ref[pl.ds(k * CHUNK, CHUNK + HALO), x_lanes].astype(f32)
+                wide = x_ref[pl.ds(k * CHUNK, CHUNK + HALO), lanes].astype(f32)
                 total = wx_ref[4:5, lanes] + wx_ref[3:4, lanes] * wide[HALO:]
                 for d in range(1, 4):
                     total += (
@@ -250,6 +268,18 @@
             target = lax.rem(me + distance, size)
             hop(back_s.at[target], inc_s.at[me], distance, bsend_sem, brecv_sem).start()
         inc_s[me] = back_s[me]
+        rows_copy.wait()
+        for n in range(width // gate_tile):
+            gate_copy(n).wait()
+
+        @pl.loop(0, width // gate_tile)
+        def _(n):
+            at = pl.ds(pl.multiple_of(n * gate_tile, gate_tile), gate_tile)
+            gate = jnp.dot(rows_s[...], wz_s[n], preferred_element_type=f32)
+            z_s[:, at] = (
+                gate * widen(scale_ref[pl.ds(HALO, rows), :], gate_tile // LANES)
+            ).astype(bf16)
+
         for distance in range(1, size):
             source = lax.rem(me - distance + size, size)
             hop(back_s.at[me], inc_s.at[source], distance, bsend_sem, brecv_sem).wait_recv()
@@ -269,7 +299,7 @@
                 weight = jnp.dot(cw_s[here, :], pick, preferred_element_type=f32)
                 carried = jnp.dot(c_s[here, :], state.astype(bf16), preferred_element_type=f32)
                 out = y_s[here, lanes] + weight * carried
-                gate = zx_ref[pl.ds(k * CHUNK + HALO, CHUNK), lanes].astype(f32)
+                gate = z_s[here, lanes].astype(f32)
                 out = out * silu(gate)
                 square = out * out
                 sums = square[:, :LANES]
@@ -287,10 +317,13 @@
             hop(back_s.at[target], inc_s.at[me], distance, bsend_sem, brecv_sem).wait_send()
 
 
-def mixer(live, zx, bcdt, idc, idr, wx, wbc, hv):
+def mixer(live, x_raw, bcdt, scaled, scale, weight_zx, idc, idr, wx, wbc, hv):
     size = lax.axis_size("seq")
-    rows = zx.shape[0] - HALO
-    width = zx.shape[1] // 2
+    rows = x_raw.shape[0] - HALO
+    width = x_raw.shape[1]
+    features = scaled.shape[1]
+    gate_tile = min(piece_width(width), 256)
+    hbm = pl.BlockSpec(memory_space=pl.ANY)
     states = wbc.shape[1] // 2
     heads_pad = hv.shape[1]
     chunks = rows // CHUNK
@@ -303,7 +336,7 @@
             jax.ShapeDtypeStruct((rows, width), bf16),
             jax.ShapeDtypeStruct((rows, LANES), f32),
         ),
-        in_specs=[vmem] * 7,
+        in_specs=[vmem, vmem, hbm, vmem, hbm] + [vmem] * 5,
         out_specs=(vmem, vmem),
         scratch_shapes=[
             pltpu.VMEM((3, rows, LANES), f32),
@@ -326,6 +359,11 @@
             pltpu.VMEM((size, 1, width), f32),
             pltpu.VMEM((size, slab, width), bf16),
             pltpu.VMEM((size, slab, width), bf16),
+            pltpu.VMEM((rows, features), bf16),
+            pltpu.VMEM((width // gate_tile, features, gate_tile), bf16),
+            pltpu.VMEM((rows, width), bf16),
+            pltpu.SemaphoreType.DMA,
+            pltpu.SemaphoreType.DMA((width // gate_tile,)),
             dma,
             dma,
             dma,
@@ -334,10 +372,10 @@
             dma,
         ],
         compiler_params=pltpu.CompilerParams(
-            collective_id=live, has_side_effects=True, vmem_limit_bytes=56 * 1024 * 1024
+            collective_id=live, has_side_effects=True, vmem_limit_bytes=63 * 1024 * 1024
         ),
         name=f"mixer_{live}",
-    )(zx, bcdt, idc, idr, wx, wbc, hv)
+    )(x_raw, bcdt, scaled, scale, weight_zx, idc, idr, wx, wbc, hv)
 
 
 def piece_width(features):
@@ -352,16 +390,16 @@
         gated_ref, squares_ref, weight_out = take(3)
     (hidden_ref,) = take(1)
     if in_live is not None:
-        gain_ref, weight_zx, weight_small = take(3)
+        gain_ref, weight_zx, weight_bc, weight_dt = take(4)
     if out_live is not None:
         (done_ref,) = take(1)
     if in_live is not None:
-        zx_ref, small_ref = take(2)
+        x_ref, small_ref, scaled_ref, scale_ref = take(4)
     if out_live is not None:
         wo_s, part_s, psend_s, precv_s, sqsend_s, sqrecv_s = take(6)
         wo_sem, psend_sem, precv_sem, sqsend_sem, sqrecv_sem = take(5)
     if in_live is not None:
-        rows_s, wz_s, acc_s, accb_s, squares_s, gain_s = take(6)
+        rows_s, wz_s, acc_s, accb_s, squares_s = take(5)
         wz_sem, rsend_sem, rrecv_sem, hsend_sem, hrecv_sem = take(5)
 
     tp = lax.axis_size("tp")
@@ -456,7 +494,9 @@
 
     def weight_copy(c):
         return pltpu.make_async_copy(
-            weight_zx.at[pl.ds(c * piece, piece)], wz_s.at[c % 2], wz_sem.at[c % 2]
+            weight_zx.at[pl.ds(c * piece, piece), pl.ds(x_ref.shape[1], x_ref.shape[1])],
+            wz_s.at[c],
+            wz_sem.at[c],
         )
 
     def forward_rows(source, c):
@@ -481,7 +521,7 @@
                     halo_copy(source, c, target).wait_send()
 
     def project():
-        for c in range(min(2, pieces)):
+        for c in range(pieces):
             weight_copy(c).start()
         for distance in range(1 if sends_rows else 0, tp):
             greet(pipe=from_live, tp=lax.rem(t - distance + tp, tp))
@@ -503,7 +543,7 @@
             rows_s[:, pl.ds(0, HALO), :] = jnp.zeros((pieces, HALO, piece), bf16)
 
         total_rows = rows_s.shape[1]
-        out_cols = zx_ref.shape[1]
+        out_cols = x_ref.shape[1]
         tile = piece_width(out_cols)
         squares_s[...] = jnp.zeros_like(squares_s)
         for c in range(pieces):
@@ -521,38 +561,45 @@
             for i in range(1, piece // LANES):
                 sums += square[:, i * LANES : (i + 1) * LANES]
             squares_s[...] += sums
-            gain_s[...] = (values * gain_ref[0:1, cols(c)]).astype(bf16)
+            scaled_ref[:, cols(c)] = (values * gain_ref[0:1, cols(c)]).astype(bf16)
             last = c == pieces - 1
             if last:
                 mean = jnp.sum(squares_s[...], axis=1, keepdims=True) / features
-                squares_s[...] = jnp.broadcast_to(
+                scale_ref[...] = jnp.broadcast_to(
                     lax.rsqrt(mean + epsilon), (total_rows, LANES)
                 )
-            small = jnp.dot(
-                gain_s[...], weight_small[pl.ds(c * piece, piece), :], preferred_element_type=f32
-            )
-            if c > 0:
-                small += accb_s[...]
-            if last:
-                small_ref[...] = small * squares_s[:, 0:1]
-            else:
-                accb_s[...] = small
+            start = 0
+            for weight in (weight_bc, weight_dt):
+                at = slice(start, start + weight.shape[1])
+                start += weight.shape[1]
+                small = jnp.dot(
+                    scaled_ref[:, cols(c)],
+                    weight[pl.ds(c * piece, piece), :],
+                    preferred_element_type=f32,
+                )
+                if c > 0:
+                    small += accb_s[:, at]
+                if last:
+                    small_ref[:, at] = small * widen(scale_ref[...], small.shape[1] // LANES)
+                else:
+                    accb_s[:, at] = small
 
             @pl.loop(0, out_cols // tile)
             def _(n):
                 at = pl.ds(pl.multiple_of(n * tile, tile), tile)
                 value = jnp.dot(
-                    gain_s[...], wz_s[c % 2, :, at], preferred_element_type=f32
+                    scaled_ref[:, cols(c)], wz_s[c, :, at], preferred_element_type=f32
                 )
                 if c > 0:
                     value += acc_s[:, at]
                 if last:
-                    zx_ref[:, at] = (value * widen(squares_s[...], tile // LANES)).astype(bf16)
+                    x_ref[:, at] = (value * widen(scale_ref[...], tile // LANES)).astype(bf16)
                 else:
                     acc_s[:, at] = value
 
-            if c + 2 < pieces:
-                weight_copy(c + 2).start()
+            if not sends_rows:
+                mine = pl.ds(pl.multiple_of(HALO + t * count, HALO), count)
+                done_ref[:, cols(c)] = rows_s[c, mine, :]
         if sends_rows:
             drain_rows(hidden_ref)
 
@@ -619,6 +666,14 @@
         pl.when(pipe == out_live)(finish)
     if in_live is not None:
         pl.when(pipe == in_live)(project)
+    if out_live is not None:
+        idle = pipe != out_live
+        if in_live is not None:
+            idle = idle & (pipe != in_live)
+
+        @pl.when(idle)
+        def _():
+            done_ref[...] = hidden_ref[...]
 
 
 def boundary(out_live, in_live, out_args, hidden, in_args):
@@ -638,7 +693,7 @@
     specs.append(vmem)
     if in_live is not None:
         args += in_args
-        specs += [vmem, hbm, vmem]
+        specs += [vmem, hbm, vmem, vmem]
     if out_live is not None:
         outs.append(jax.ShapeDtypeStruct((count, features), bf16))
         width = out_args[2].shape[0]
@@ -657,19 +712,21 @@
         ]
     if in_live is not None:
         rows = HALO + tp * count
-        wide, small = in_args[1].shape[1], in_args[2].shape[1]
+        wide = in_args[1].shape[1] // 2
+        small = in_args[2].shape[1] + in_args[3].shape[1]
         outs += [
             jax.ShapeDtypeStruct((rows, wide), bf16),
             jax.ShapeDtypeStruct((rows, small), f32),
+            jax.ShapeDtypeStruct((rows, features), bf16),
+            jax.ShapeDtypeStruct((rows, LANES), f32),
         ]
         scratch += [
             pltpu.VMEM((pieces, rows, piece), bf16),
-            pltpu.VMEM((2, piece, wide), bf16),
+            pltpu.VMEM((pieces, piece, wide), bf16),
             pltpu.VMEM((rows, wide), f32),
             pltpu.VMEM((rows, small), f32),
             pltpu.VMEM((rows, LANES), f32),
-            pltpu.VMEM((rows, piece), bf16),
-            dma((2,)),
+            dma((pieces,)),
             dma((pieces, tp)),
             dma((pieces, tp)),
             dma((pieces, tp)),
@@ -710,15 +767,12 @@
     out_w,
 ):
     sections = lax.axis_size("pipe")
-    section_index = lax.axis_index("pipe")
     local_width = gated_gain.shape[1]
     heads = dt_bias.shape[1]
     head_width = local_width // heads
     heads_pad = -(-heads // LANES) * LANES
     weight_zx = in_zx[0].reshape(in_zx.shape[1], 2 * local_width)
-    weight_small = jnp.concatenate(
-        [in_bc[0], jnp.pad(in_dt[0], ((0, 0), (0, heads_pad - heads)))], 1
-    )
+    weight_dt = jnp.pad(in_dt[0], ((0, 0), (0, heads_pad - heads)))
     wx = jnp.concatenate(
         [
             conv_x[0],
@@ -744,20 +798,17 @@
     idc = jnp.broadcast_to(ids_ext[:, None], (ids_ext.shape[0], LANES))
     idr = jnp.broadcast_to(row_ids[None, :], (8, row_ids.shape[0]))
     gain = jnp.broadcast_to(norm_gain, (8, norm_gain.shape[1]))
-    in_args = [gain, weight_zx, weight_small]
-    zx, bcdt = boundary(None, 0, None, hidden_in[0], in_args)
+    in_args = [gain, weight_zx, in_bc[0], weight_dt]
+    projected = boundary(None, 0, None, hidden_in[0], in_args)
     current = hidden_in[0]
-    finished = None
     for live in range(sections):
-        gated, squares = mixer(live, zx, bcdt, idc, idr, wx, wbc, hv)
+        gated, squares = mixer(live, *projected, weight_zx, idc, idr, wx, wbc, hv)
         out_args = [gated, squares, out_w[0]]
         if live + 1 < sections:
-            done, zx, bcdt = boundary(live, live + 1, out_args, current, in_args)
-            current = lax.ppermute(done, "pipe", [(live, live + 1)])
+            current, *projected = boundary(live, live + 1, out_args, current, in_args)
         else:
-            (done,) = boundary(live, None, out_args, current, None)
-        finished = done if live == 0 else jnp.where(section_index == live, done, finished)
-    return finished[None, None]
+            (current,) = boundary(live, None, out_args, current, None)
+    return current[None, None]
 
 
 def solution(mesh):

time: 220 us -> 197 us (0.90)
  Pallas kernels: 187 us -> 164 us
  local copies, waits for them, and re-layouts: 21.7 us -> 26.4 us
  other arithmetic: 6.21 us -> 2.8 us
    pallas_call x3, Pallas kernels: 146 us -> 126 us  [boundary(): pl.pallas_call(functools.partial(boundary_kernel, out_live, in_live), out...]
    unnamed x24 -> x17, local copies, waits for them, and re-layouts: 18.7 us -> 21.8 us
    broadcast_in_dim x1 -> x0, other arithmetic: 2.52 us -> none  [local(): return finished[None, None]]
  transfers between devices with their start and end apart: 2 -> 1, of which waited for: 0 -> 0; matrix products, arithmetic and copies ran while one was open for 10% -> 12% of each run, Pallas kernels for 18% -> 3%
where the time goes in v2:
time: 197 us
  Pallas kernels  164 us (83%)
  local copies, waits for them, and re-layouts  26.4 us (13%)
  starting transfers between devices  3.16 us (2%)
  other arithmetic  2.8 us (1%)
    pallas_call x3, Pallas kernels, boundary(): pl.pallas_call(functools.partial(boundary_kernel, out_live, in_live), out...  126 us
    pallas_call x2, Pallas kernels, mixer(): pl.pallas_call(functools.partial(mixer_kernel, live), out_shape=(jax.Shap...  38.7 us
    unnamed x17, local copies, waits for them, and re-layouts  21.8 us
  transfers between devices with their start and end apart: 1, of which 0 were waited for; matrix products, arithmetic and copies ran while one was open for 12% of the time, Pallas kernels for 3%

profile of v2, /device:TPU:11, one launch (start us, length us, event | category | flops | bytes accessed | tf_op | source)
XLA Modules:
  0.0 197.0 jit_solution(11993880754601555328)
XLA Ops:
  0.0 0.7 convert_element_type.11
  0.7 0.1 fusion
  0.8 3.2 %collective-permute-start = (f32[16]{0:T(128)S(1)}, f32[16]{0:T(128)S(1)}, u32[]{:S(2)}, u32[]{:S(2)}) collective-permute-start(f32[16]{0:T(128)S(1)} %fusion), channel_id=1, source_target_pairs={{0,2},{2,4},{4,6},{6,8},{8,10},{10,12},{12,14},{1,3},{3,5},{5,7},{... | collective-permute-start | bytes 200 | tf_op jit(solution)/shard_map/ppermute | solution.py:792
  3.9 0.7 negate_multiply_fusion
  4.6 0.7 broadcast_in_dim.37
  5.3 0.1 broadcast_in_dim.38
  5.4 1.3 copy.16
  6.7 0.0 copy-start.6
  6.7 0.0 copy-start.3
  6.7 0.0 copy-start.4
  6.7 0.0 copy-start.5
  6.7 0.0 copy-start
  6.7 0.0 copy-start.1
  6.7 0.0 copy-start.2
  6.8 18.0 %copy.17 = bf16[320,8,2,2560]{3,1,2,0:T(8,128)(2,1)} copy(bf16[320,8,2,2560]{3,2,1,0:T(2,128)(2,1)} %bitcast.20) | data formatting | bytes 52428800
  24.8 0.1 pad.14.clone
  24.8 0.0 copy-done.6
  24.9 0.6 select_maximum_fusion.hv_ref
  25.4 0.0 copy-done.3
  25.5 1.0 pad.8.refs_4_.refs_7_
  26.4 0.0 copy-done.4
  26.4 0.0 copy-done.5
  26.5 0.7 maximum_maximum_fusion.wbc_ref
  27.1 0.0 copy-done
  27.1 0.0 copy-done.1
  27.1 0.0 copy-done.2
  27.2 0.7 concatenate.13.wx_ref
  27.9 0.6 broadcast_in_dim.34.refs_1_.refs_4_
  28.5 5.0 %boundary_0.1 = (bf16[528,2560]{1,0:T(8,128)(2,1)}, f32[528,384]{1,0:T(8,128)}, bf16[528,2560]{1,0:T(8,128)(2,1)}, f32[528,128]{1,0:T(8,128)}) custom-call(bf16[256,2560]{1,0:T(8,128)(2,1)} %bitcast.22, f32[8,2560]{1,0:T(8,128)} %broadcast_in_dim.34.refs_1_.refs_4_, bf16[2560,5120]{1,0:T(8,128)(2,1)} %bitcast.14, bf16[2560,256]{1,0:T(8,128)(2,1)} %bitcast.24, ...), custom_call_target="tpu_custom_call" | custom-call | tf_op jit(solution)/shard_map/boundary_0/pallas_call | solution.py:737
  33.6 0.0 collective-permute-done
  33.6 0.1 pad_maximum_fusion
  33.7 0.6 broadcast_in_dim.36.idr_ref
  34.3 0.8 broadcast_in_dim.35.idc_ref
  35.1 4.2 %mixer_0.1 = (bf16[512,2560]{1,0:T(8,128)(2,1)}, f32[512,128]{1,0:T(8,128)}) custom-call(bf16[528,2560]{1,0:T(8,128)(2,1)} %get-tuple-element.18.x_ref, f32[528,384]{1,0:T(8,128)} %get-tuple-element.19.bcdt_ref, bf16[528,2560]{1,0:T(8,128)(2,1)} %get-tuple-element.20.scaled_ref, f32[528,128]{1,0:T(8,128)} %get-tuple-element.21.scale_ref, ...), custom_call_target="tpu_custom_call" | custom-call | tf_op jit(solution)/shard_map/mixer_0/pallas_call | solution.py:333
  39.3 97.5 %boundary_1.1 = (bf16[256,2560]{1,0:T(8,128)(2,1)}, bf16[528,2560]{1,0:T(8,128)(2,1)}, f32[528,384]{1,0:T(8,128)}, bf16[528,2560]{1,0:T(8,128)(2,1)}, f32[528,128]{1,0:T(8,128)}) custom-call(bf16[512,2560]{1,0:T(8,128)(2,1)} %get-tuple-element.22.refs_0_, f32[512,128]{1,0:T(8,128)} %get-tuple-element.23.refs_1_, bf16[2560,2560]{1,0:T(8,128)(2,1)} %bitcast.18, ...), custom_call_target="tpu_custom_call" | custom-call | tf_op jit(solution)/shard_map/boundary_1/pallas_call | solution.py:737
  136.8 34.5 %mixer_1.1 = (bf16[512,2560]{1,0:T(8,128)(2,1)}, f32[512,128]{1,0:T(8,128)}) custom-call(bf16[528,2560]{1,0:T(8,128)(2,1)} %get-tuple-element.24.x_ref, f32[528,384]{1,0:T(8,128)} %get-tuple-element.25.bcdt_ref, bf16[528,2560]{1,0:T(8,128)(2,1)} %get-tuple-element.26.scaled_ref, f32[528,128]{1,0:T(8,128)} %get-tuple-element.27.scale_ref, ...), custom_call_target="tpu_custom_call" | custom-call | tf_op jit(solution)/shard_map/mixer_1/pallas_call | solution.py:333
  171.4 23.2 %boundary_2.1 = bf16[256,2560]{1,0:T(8,128)(2,1)} custom-call(bf16[512,2560]{1,0:T(8,128)(2,1)} %get-tuple-element.28.refs_0_, f32[512,128]{1,0:T(8,128)} %get-tuple-element.29.refs_1_, bf16[2560,2560]{1,0:T(8,128)(2,1)} %bitcast.19, bf16[256,2560]{1,0:T(8,128)(2,1)} %get-tuple-element.30.refs_3_), custom_call_target="tpu_custom_call" | custom-call | tf_op jit(solution)/shard_map/boundary_2/pallas_call | solution.py:737
  194.6 2.5 %copy.19 = bf16[1,1,256,2560]{3,2,1,0:T(8,128)(2,1)} copy(bf16[1,1,256,2560]{3,2,1,0:T(8,128)(2,1)} %bitcast.21) | data formatting | bytes 2621440
  (4 shorter events, 0.0 us)
Async XLA Ops:
  0.8 32.8 %collective-permute-start = (f32[16]{0:T(128)S(1)}, f32[16]{0:T(128)S(1)}, u32[]{:S(2)}, u32[]{:S(2)}) collective-permute-start(f32[16]{0:T(128)S(1)} %fusion), channel_id=1, source_target_pairs={{0,2},{2,4},{4,6},{6,8},{8,10},{10,12},{12,14},{1,3},{3,5},{5,7},{... | collective-permute-start | bytes 200 | tf_op jit(solution)/shard_map/ppermute | solution.py:792
  6.7 18.2 %copy-start.6 = (f32[1,40]{1,0:T(1,128)S(1)}, f32[1,40]{1,0:T(1,128)}, u32[]{:S(2)}) copy-start(f32[1,40]{1,0:T(1,128)} %param.25) | copy-start | bytes 484
  6.7 18.8 %copy-start.3 = (f32[1,2560]{1,0:T(1,128)S(1)}, f32[1,2560]{1,0:T(1,128)}, u32[]{:S(2)}) copy-start(f32[1,2560]{1,0:T(1,128)} %param.17) | copy-start | bytes 30724
  6.7 19.8 %copy-start.4 = (f32[1,4,256]{2,1,0:T(4,128)S(1)}, f32[1,4,256]{2,1,0:T(4,128)}, u32[]{:S(2)}) copy-start(f32[1,4,256]{2,1,0:T(4,128)} %param.22) | copy-start | bytes 12292
  6.7 19.7 %copy-start.5 = (f32[1,256]{1,0:T(1,128)S(1)}, f32[1,256]{1,0:T(1,128)}, u32[]{:S(2)}) copy-start(f32[1,256]{1,0:T(1,128)} %param.24) | copy-start | bytes 3076
  6.7 20.4 %copy-start = (f32[1,4,2560]{2,1,0:T(4,128)S(1)}, f32[1,4,2560]{2,1,0:T(4,128)}, u32[]{:S(2)}) copy-start(f32[1,4,2560]{2,1,0:T(4,128)} %param.21) | copy-start | bytes 122884
  6.7 20.4 %copy-start.1 = (f32[1,2560]{1,0:T(1,128)S(1)}, f32[1,2560]{1,0:T(1,128)}, u32[]{:S(2)}) copy-start(f32[1,2560]{1,0:T(1,128)} %param.23) | copy-start | bytes 30724
  6.7 20.4 %copy-start.2 = (f32[1,2560]{1,0:T(1,128)S(1)}, f32[1,2560]{1,0:T(1,128)}, u32[]{:S(2)}) copy-start(f32[1,2560]{1,0:T(1,128)} %param.28) | copy-start | bytes 30724

commit v3 on v2

--- a/solution.py
+++ b/solution.py
@@ -41,8 +41,11 @@
     weight_zx,
     idc_ref,
     idr_ref,
-    wx_ref,
-    wbc_ref,
+    cx_ref,
+    bx_ref,
+    gg_ref,
+    cb_ref,
+    bb_ref,
     hv_ref,
     g_ref,
     ss_ref,
@@ -102,12 +105,19 @@
         hit = lax.rem(row_iota(shape), heads_pad) == tile * 2 + lane_iota(shape) // head_width
         return hit.astype(f32).astype(dtype)
 
-    def hop(source, target_ref, distance, send, recv):
+    turns = tiles // group
+    middle = turns // 2
+    halves = [(0, middle), (middle, turns)]
+    cuts = [0, turns * 3 // 10, turns * 6 // 10, turns]
+
+    def hop(source, target_ref, half, distance, send, recv):
+        first, end = halves[half]
+        cols = pl.ds(first * span, (end - first) * span)
         return pltpu.make_async_remote_copy(
-            src_ref=source,
-            dst_ref=target_ref,
-            send_sem=send.at[distance - 1],
-            recv_sem=recv.at[distance - 1],
+            src_ref=source.at[:, cols],
+            dst_ref=target_ref.at[:, cols],
+            send_sem=send.at[half, distance - 1],
+            recv_sem=recv.at[half, distance - 1],
             device_id={"seq": lax.rem(me + distance, size)},
             device_id_type=MESH,
         )
@@ -117,7 +127,7 @@
         barrier = pltpu.get_barrier_semaphore()
         rows_copy = pltpu.make_async_copy(scaled_ref.at[pl.ds(HALO, rows)], rows_s, rows_sem)
         rows_copy.start()
-        gate_tile = wz_s.shape[2]
+        gate_tile = span
 
         def gate_copy(n):
             return pltpu.make_async_copy(
@@ -138,6 +148,8 @@
         lower = row_iota(square_shape) >= lane_iota(square_shape)
         lower_f = lower.astype(f32)
         keep_s[...] = jnp.zeros_like(keep_s)
+        keep_s[chunks : chunks + 1, :] = hv_ref[2:3, :]
+        rate = jnp.exp(hv_ref[1:2, :]) * -LOG2E
 
         @pl.loop(0, chunks)
         def _(k):
@@ -154,7 +166,7 @@
             step = jnp.maximum(raw, 0.0) + jnp.log1p(jnp.exp(-jnp.abs(raw)))
             level = jnp.dot(
                 lower_f,
-                step * hv_ref[1:2, :],
+                step * rate,
                 precision=lax.Precision.HIGHEST,
                 preferred_element_type=f32,
             )
@@ -171,11 +183,11 @@
             for half in range(2):
                 cols = pl.ds(half * states, states)
                 wide = bcdt_ref[pl.ds(base, CHUNK + HALO), cols]
-                total = wbc_ref[4:5, cols] + wbc_ref[3:4, cols] * wide[HALO:]
+                total = bb_ref[0:1, cols] + cb_ref[3:4, cols] * wide[HALO:]
                 for d in range(1, 4):
                     total += (
                         mask_s[d - 1, here, :]
-                        * wbc_ref[3 - d : 4 - d, cols]
+                        * cb_ref[3 - d : 4 - d, cols]
                         * pltpu.roll(wide, d, 0)[HALO:]
                     )
                 place = b_s if half == 0 else c_s
@@ -186,8 +198,7 @@
             same_doc = seg == idr_ref[0:1, pl.ds(base, CHUNK)]
             gm_s[k] = jnp.where(lower & same_doc, gram, 0.0)
 
-        @pl.loop(0, tiles // group)
-        def _(turn):
+        def enter(turn):
             tile = turn * group
             lanes = pl.ds(pl.multiple_of(turn * span, span), span)
             pick = selector(tile, 2 * heads_pad, bf16)
@@ -198,11 +209,11 @@
             for k in range(chunks):
                 here = pl.ds(k * CHUNK, CHUNK)
                 wide = x_ref[pl.ds(k * CHUNK, CHUNK + HALO), lanes].astype(f32)
-                total = wx_ref[4:5, lanes] + wx_ref[3:4, lanes] * wide[HALO:]
+                total = bx_ref[0:1, lanes] + cx_ref[3:4, lanes] * wide[HALO:]
                 for d in range(1, 4):
                     total += (
                         widen(mask_s[d - 1, here, :], group)
-                        * wx_ref[3 - d : 4 - d, lanes]
+                        * cx_ref[3 - d : 4 - d, lanes]
                         * pltpu.roll(wide, d, 0)[HALO:]
                     )
                 conv = silu(total)
@@ -222,16 +233,7 @@
                 send_s[part, :, lanes] = state[part * slab : (part + 1) * slab].astype(bf16)
             ksend_s[:, lanes] = keep_all
 
-        pl.semaphore_wait(barrier, size - 1)
-        for distance in range(1, size):
-            target = lax.rem(me + distance, size)
-            hop(send_s.at[target], recv_s.at[me], distance, send_sem, recv_sem).start()
-            hop(ksend_s, krecv_s.at[me], distance, ksend_sem, krecv_sem).start()
-        recv_s[me] = send_s[me]
-        krecv_s[me] = ksend_s[...]
-
-        @pl.loop(0, tiles // group)
-        def _(turn):
+        def inside(turn):
             first_half = lane_iota((CHUNK, LANES)) < head_width
             for k in range(chunks):
                 here = pl.ds(k * CHUNK, CHUNK)
@@ -253,41 +255,13 @@
                     out = jnp.dot(
                         jnp.concatenate(mixes, 1), both, preferred_element_type=f32
                     )
-                    y_s[here, lanes] = out + wx_ref[5:6, lanes] * conv.astype(f32)
-
-        for distance in range(1, size):
-            source = lax.rem(me - distance + size, size)
-            hop(send_s.at[me], recv_s.at[source], distance, send_sem, recv_sem).wait_recv()
-            hop(ksend_s, krecv_s.at[source], distance, ksend_sem, krecv_sem).wait_recv()
-        run = jnp.zeros((slab, width), f32)
-        for part in range(size):
-            back_s[part] = run.astype(bf16)
-            if part < size - 1:
-                run = run * krecv_s[part] + recv_s[part].astype(f32)
-        for distance in range(1, size):
-            target = lax.rem(me + distance, size)
-            hop(back_s.at[target], inc_s.at[me], distance, bsend_sem, brecv_sem).start()
-        inc_s[me] = back_s[me]
-        rows_copy.wait()
-        for n in range(width // gate_tile):
-            gate_copy(n).wait()
-
-        @pl.loop(0, width // gate_tile)
-        def _(n):
-            at = pl.ds(pl.multiple_of(n * gate_tile, gate_tile), gate_tile)
-            gate = jnp.dot(rows_s[...], wz_s[n], preferred_element_type=f32)
-            z_s[:, at] = (
-                gate * widen(scale_ref[pl.ds(HALO, rows), :], gate_tile // LANES)
-            ).astype(bf16)
-
-        for distance in range(1, size):
-            source = lax.rem(me - distance + size, size)
-            hop(back_s.at[me], inc_s.at[source], distance, bsend_sem, brecv_sem).wait_recv()
-
-        ss_ref[...] = jnp.zeros_like(ss_ref)
-
-        @pl.loop(0, tiles // group)
-        def _(turn):
+                    y_s[here, lanes] = out + keepx_s[chunks : chunks + 1, lanes] * conv.astype(f32)
+            gate_copy(turn).wait()
+            at = pl.ds(pl.multiple_of(turn * span, span), span)
+            gate = jnp.dot(rows_s[...], wz_s[turn], preferred_element_type=f32)
+            z_s[:, at] = (gate * widen(scale_ref[pl.ds(HALO, rows), :], group)).astype(bf16)
+
+        def leave(turn):
             lanes = pl.ds(pl.multiple_of(turn * span, span), span)
             pick = selector(turn * group, 2 * heads_pad, bf16)
             keeps = keepx_s[:, lanes]
@@ -306,37 +280,85 @@
                 for i in range(1, group):
                     sums += square[:, i * LANES : (i + 1) * LANES]
                 ss_ref[here, :] += sums
-                g_ref[here, lanes] = (out * wx_ref[6:7, lanes]).astype(bf16)
+                g_ref[here, lanes] = (out * gg_ref[0:1, lanes]).astype(bf16)
                 if k < chunks - 1:
                     state = state * keeps[k : k + 1] + fresh_s[k, :, lanes]
 
-        for distance in range(1, size):
-            target = lax.rem(me + distance, size)
-            hop(send_s.at[target], recv_s.at[me], distance, send_sem, recv_sem).wait_send()
-            hop(ksend_s, krecv_s.at[me], distance, ksend_sem, krecv_sem).wait_send()
-            hop(back_s.at[target], inc_s.at[me], distance, bsend_sem, brecv_sem).wait_send()
-
-
-def mixer(live, x_raw, bcdt, scaled, scale, weight_zx, idc, idr, wx, wbc, hv):
+        def send_half(half):
+            for distance in range(1, size):
+                target = lax.rem(me + distance, size)
+                hop(send_s.at[target], recv_s.at[me], half, distance, send_sem, recv_sem).start()
+                hop(ksend_s, krecv_s.at[me], half, distance, ksend_sem, krecv_sem).start()
+
+        def scan_half(half):
+            for distance in range(1, size):
+                source = lax.rem(me - distance + size, size)
+                hop(send_s.at[me], recv_s.at[source], half, distance, send_sem, recv_sem).wait_recv()
+                hop(ksend_s, krecv_s.at[source], half, distance, ksend_sem, krecv_sem).wait_recv()
+            first, end = halves[half]
+            cols = slice(first * span, end * span)
+            run = jnp.zeros((slab, (end - first) * span), f32)
+            for part in range(size):
+                back_s[part, :, cols] = run.astype(bf16)
+                if part < size - 1:
+                    run = run * krecv_s[part, :, cols] + recv_s[part, :, cols].astype(f32)
+            for distance in range(1, size):
+                target = lax.rem(me + distance, size)
+                hop(back_s.at[target], inc_s.at[me], half, distance, bsend_sem, brecv_sem).start()
+            inc_s[me, :, cols] = back_s[me, :, cols]
+
+        def leave_half(half):
+            for distance in range(1, size):
+                source = lax.rem(me - distance + size, size)
+                hop(back_s.at[me], inc_s.at[source], half, distance, bsend_sem, brecv_sem).wait_recv()
+            pl.loop(*halves[half])(leave)
+
+        pl.loop(*halves[0])(enter)
+        pl.semaphore_wait(barrier, size - 1)
+        send_half(0)
+        pl.loop(*halves[1])(enter)
+        send_half(1)
+        recv_s[me] = send_s[me]
+        krecv_s[me] = ksend_s[...]
+        ss_ref[...] = jnp.zeros_like(ss_ref)
+        rows_copy.wait()
+        for i in range(3):
+            if cuts[i] < cuts[i + 1]:
+                pl.loop(cuts[i], cuts[i + 1])(inside)
+            if i < 2:
+                scan_half(i)
+        for half in range(2):
+            leave_half(half)
+
+        for half in range(2):
+            for distance in range(1, size):
+                target = lax.rem(me + distance, size)
+                hop(send_s.at[target], recv_s.at[me], half, distance, send_sem, recv_sem).wait_send()
+                hop(ksend_s, krecv_s.at[me], half, distance, ksend_sem, krecv_sem).wait_send()
+                hop(back_s.at[target], inc_s.at[me], half, distance, bsend_sem, brecv_sem).wait_send()
+
+
+def mixer(live, x_raw, bcdt, scaled, scale, weight_zx, idc, idr, cx, bx, gg, cb, bb, hv):
     size = lax.axis_size("seq")
     rows = x_raw.shape[0] - HALO
     width = x_raw.shape[1]
     features = scaled.shape[1]
-    gate_tile = min(piece_width(width), 256)
+    gate_tile = 2 * LANES if width % (2 * LANES) == 0 else LANES
+    keeps = -(-(rows // CHUNK + 1) // 8) * 8
     hbm = pl.BlockSpec(memory_space=pl.ANY)
-    states = wbc.shape[1] // 2
+    states = cb.shape[1] // 2
     heads_pad = hv.shape[1]
     chunks = rows // CHUNK
     slab = states // size
     vmem = pl.BlockSpec(memory_space=pltpu.VMEM)
-    dma = pltpu.SemaphoreType.DMA((size - 1,))
+    dma = pltpu.SemaphoreType.DMA((2, size - 1))
     return pl.pallas_call(
         functools.partial(mixer_kernel, live),
         out_shape=(
             jax.ShapeDtypeStruct((rows, width), bf16),
             jax.ShapeDtypeStruct((rows, LANES), f32),
         ),
-        in_specs=[vmem, vmem, hbm, vmem, hbm] + [vmem] * 5,
+        in_specs=[vmem, vmem, hbm, vmem, hbm] + [vmem] * 8,
         out_specs=(vmem, vmem),
         scratch_shapes=[
             pltpu.VMEM((3, rows, LANES), f32),
@@ -345,8 +367,8 @@
             pltpu.VMEM((chunks, heads_pad, CHUNK), f32),
             pltpu.VMEM((rows, 2 * heads_pad), bf16),
             pltpu.VMEM((rows, 2 * heads_pad), bf16),
-            pltpu.VMEM((8, heads_pad), f32),
-            pltpu.VMEM((8, width), f32),
+            pltpu.VMEM((keeps, heads_pad), f32),
+            pltpu.VMEM((keeps, width), f32),
             pltpu.VMEM((rows, states), bf16),
             pltpu.VMEM((rows, states), bf16),
             pltpu.VMEM((chunks, CHUNK, CHUNK), f32),
@@ -375,7 +397,7 @@
             collective_id=live, has_side_effects=True, vmem_limit_bytes=63 * 1024 * 1024
         ),
         name=f"mixer_{live}",
-    )(x_raw, bcdt, scaled, scale, weight_zx, idc, idr, wx, wbc, hv)
+    )(x_raw, bcdt, scaled, scale, weight_zx, idc, idr, cx, bx, gg, cb, bb, hv)
 
 
 def piece_width(features):
@@ -769,24 +791,11 @@
     sections = lax.axis_size("pipe")
     local_width = gated_gain.shape[1]
     heads = dt_bias.shape[1]
-    head_width = local_width // heads
     heads_pad = -(-heads // LANES) * LANES
     weight_zx = in_zx[0].reshape(in_zx.shape[1], 2 * local_width)
     weight_dt = jnp.pad(in_dt[0], ((0, 0), (0, heads_pad - heads)))
-    wx = jnp.concatenate(
-        [
-            conv_x[0],
-            bias_x,
-            jnp.repeat(d_skip, head_width, axis=1),
-            gated_gain,
-            jnp.zeros_like(gated_gain),
-        ],
-        0,
-    )
-    wbc = jnp.concatenate([conv_bc[0], bias_bc, jnp.zeros((3, bias_bc.shape[1]), f32)], 0)
     hv = jnp.pad(
-        jnp.concatenate([dt_bias, -jnp.exp(a_log) * LOG2E], 0),
-        ((0, 6), (0, heads_pad - heads)),
+        jnp.concatenate([dt_bias, a_log, d_skip], 0), ((0, 0), (0, heads_pad - heads))
     )
     row_ids = doc_ids[0].astype(f32)
     edge = lax.ppermute(
@@ -796,13 +805,24 @@
     )
     ids_ext = jnp.concatenate([edge - 1.0, row_ids])
     idc = jnp.broadcast_to(ids_ext[:, None], (ids_ext.shape[0], LANES))
-    idr = jnp.broadcast_to(row_ids[None, :], (8, row_ids.shape[0]))
-    gain = jnp.broadcast_to(norm_gain, (8, norm_gain.shape[1]))
-    in_args = [gain, weight_zx, in_bc[0], weight_dt]
+    idr = row_ids[None, :]
+    in_args = [norm_gain, weight_zx, in_bc[0], weight_dt]
     projected = boundary(None, 0, None, hidden_in[0], in_args)
     current = hidden_in[0]
     for live in range(sections):
-        gated, squares = mixer(live, *projected, weight_zx, idc, idr, wx, wbc, hv)
+        gated, squares = mixer(
+            live,
+            *projected,
+            weight_zx,
+            idc,
+            idr,
+            conv_x[0],
+            bias_x,
+            gated_gain,
+            conv_bc[0],
+            bias_bc,
+            hv,
+        )
         out_args = [gated, squares, out_w[0]]
         if live + 1 < sections:
             current, *projected = boundary(live, live + 1, out_args, current, in_args)

time: 197 us -> 190 us (0.964)
  local copies, waits for them, and re-layouts: 26.4 us -> 23.6 us
  Pallas kernels: 164 us -> 162 us
    pallas_call x3, Pallas kernels: 126 us -> 123 us  [boundary(): pl.pallas_call(functools.partial(boundary_kernel, out_live, in_live), out...]
    broadcast_in_dim x6 -> x0, local copies, waits for them, and re-layouts: 2.06 us -> none  [the longest x2 0.81 us: local(): jnp.repeat(d_skip, head_width, axis=1)]
    unnamed x17 -> x11, local copies, waits for them, and re-layouts: 21.8 us -> 21.7 us
  transfers between devices with their start and end apart: 1 -> 1, of which waited for: 0 -> 0; matrix products, arithmetic and copies ran while one was open for 12% -> 11% of each run, Pallas kernels for 3% -> 3%
where the time goes in v3:
time: 190 us
  Pallas kernels  162 us (85%)
  local copies, waits for them, and re-layouts  23.6 us (12%)
  starting transfers between devices  3.16 us (2%)
    pallas_call x3, Pallas kernels, boundary(): pl.pallas_call(functools.partial(boundary_kernel, out_live, in_live), out...  123 us
    pallas_call x2, Pallas kernels, mixer(): pl.pallas_call(functools.partial(mixer_kernel, live), out_shape=(jax.Shap...  38.7 us
    unnamed x11, local copies, waits for them, and re-layouts  21.7 us
  transfers between devices with their start and end apart: 1, of which 0 were waited for; matrix products, arithmetic and copies ran while one was open for 11% of the time, Pallas kernels for 3%

profile of v3, /device:TPU:11, one launch (start us, length us, event | category | flops | bytes accessed | tf_op | source)
XLA Modules:
  0.0 190.1 jit_solution(8003161239946326746)
XLA Ops:
  0.0 0.7 convert_element_type.11.idr_ref
  0.7 0.0 copy-start
  0.7 0.1 fusion
  0.8 3.2 %collective-permute-start = (f32[16]{0:T(128)S(1)}, f32[16]{0:T(128)S(1)}, u32[]{:S(2)}, u32[]{:S(2)}) collective-permute-start(f32[16]{0:T(128)S(1)} %fusion), channel_id=1, source_target_pairs={{0,2},{2,4},{4,6},{6,8},{8,10},{10,12},{12,14},{1,3},{3,5},{5,7},{... | collective-permute-start | bytes 200 | tf_op jit(solution)/shard_map/ppermute | solution.py:801
  3.9 1.3 copy.16
  5.2 0.0 copy-start.1
  5.2 0.0 copy-start.2
  5.2 0.0 copy-start.3
  5.2 18.0 %copy.17 = bf16[320,8,2,2560]{3,1,2,0:T(8,128)(2,1)} copy(bf16[320,8,2,2560]{3,2,1,0:T(2,128)(2,1)} %bitcast.19) | data formatting | bytes 52428800
  23.2 1.0 pad.8.refs_4_.refs_7_
  24.2 0.0 copy-done.1
  24.2 0.0 copy-done.2
  24.2 0.0 copy-done.3
  24.2 0.6 select_maximum_fusion.hv_ref
  24.8 5.0 %boundary_0.1 = (bf16[528,2560]{1,0:T(8,128)(2,1)}, f32[528,384]{1,0:T(8,128)}, bf16[528,2560]{1,0:T(8,128)(2,1)}, f32[528,128]{1,0:T(8,128)}) custom-call(bf16[256,2560]{1,0:T(8,128)(2,1)} %bitcast.20, f32[1,2560]{1,0:T(1,128)} %refs_4_.1, bf16[2560,5120]{1,0:T(8,128)(2,1)} %bitcast.13, bf16[2560,256]{1,0:T(8,128)(2,1)} %bitcast.22, ...), custom_call_target="tpu_custom_call" | custom-call | tf_op jit(solution)/shard_map/boundary_0/pallas_call | solution.py:759
  29.8 0.0 collective-permute-done
  29.8 0.0 copy-done
  29.8 0.1 pad_maximum_fusion
  29.9 0.8 broadcast_in_dim.4.idc_ref
  30.8 4.6 %mixer_0.1 = (bf16[512,2560]{1,0:T(8,128)(2,1)}, f32[512,128]{1,0:T(8,128)}) custom-call(bf16[528,2560]{1,0:T(8,128)(2,1)} %get-tuple-element.18.x_ref, f32[528,384]{1,0:T(8,128)} %get-tuple-element.19.bcdt_ref, bf16[528,2560]{1,0:T(8,128)(2,1)} %get-tuple-element.20.scaled_ref, f32[528,128]{1,0:T(8,128)} %get-tuple-element.21.scale_ref, ...), custom_call_target="tpu_custom_call" | custom-call | tf_op jit(solution)/shard_map/mixer_0/pallas_call | solution.py:355
  35.4 94.8 %boundary_1.1 = (bf16[256,2560]{1,0:T(8,128)(2,1)}, bf16[528,2560]{1,0:T(8,128)(2,1)}, f32[528,384]{1,0:T(8,128)}, bf16[528,2560]{1,0:T(8,128)(2,1)}, f32[528,128]{1,0:T(8,128)}) custom-call(bf16[512,2560]{1,0:T(8,128)(2,1)} %get-tuple-element.22.refs_0_, f32[512,128]{1,0:T(8,128)} %get-tuple-element.23.refs_1_, bf16[2560,2560]{1,0:T(8,128)(2,1)} %bitcast.17, ...), custom_call_target="tpu_custom_call" | custom-call | tf_op jit(solution)/shard_map/boundary_1/pallas_call | solution.py:759
  130.1 34.1 %mixer_1.1 = (bf16[512,2560]{1,0:T(8,128)(2,1)}, f32[512,128]{1,0:T(8,128)}) custom-call(bf16[528,2560]{1,0:T(8,128)(2,1)} %get-tuple-element.24.x_ref, f32[528,384]{1,0:T(8,128)} %get-tuple-element.25.bcdt_ref, bf16[528,2560]{1,0:T(8,128)(2,1)} %get-tuple-element.26.scaled_ref, f32[528,128]{1,0:T(8,128)} %get-tuple-element.27.scale_ref, ...), custom_call_target="tpu_custom_call" | custom-call | tf_op jit(solution)/shard_map/mixer_1/pallas_call | solution.py:355
  164.2 23.4 %boundary_2.1 = bf16[256,2560]{1,0:T(8,128)(2,1)} custom-call(bf16[512,2560]{1,0:T(8,128)(2,1)} %get-tuple-element.28.refs_0_, f32[512,128]{1,0:T(8,128)} %get-tuple-element.29.refs_1_, bf16[2560,2560]{1,0:T(8,128)(2,1)} %bitcast.18, bf16[256,2560]{1,0:T(8,128)(2,1)} %get-tuple-element.30.refs_3_), custom_call_target="tpu_custom_call" | custom-call | tf_op jit(solution)/shard_map/boundary_2/pallas_call | solution.py:759
  187.6 2.5 %copy.19 = bf16[1,1,256,2560]{3,2,1,0:T(8,128)(2,1)} copy(bf16[1,1,256,2560]{3,2,1,0:T(8,128)(2,1)} %bitcast.24) | data formatting | bytes 2621440
  (1 shorter events, 0.0 us)
Async XLA Ops:
  0.7 29.1 %copy-start = (f32[1,512]{1,0:T(1,128)}, f32[1,512]{1,0:T(1,128)S(1)}, u32[]{:S(2)}) copy-start(f32[1,512]{1,0:T(1,128)S(1)} %convert_element_type.11.idr_ref) | copy-start | bytes 6148
  0.8 29.0 %collective-permute-start = (f32[16]{0:T(128)S(1)}, f32[16]{0:T(128)S(1)}, u32[]{:S(2)}, u32[]{:S(2)}) collective-permute-start(f32[16]{0:T(128)S(1)} %fusion), channel_id=1, source_target_pairs={{0,2},{2,4},{4,6},{6,8},{8,10},{10,12},{12,14},{1,3},{3,5},{5,7},{... | collective-permute-start | bytes 200 | tf_op jit(solution)/shard_map/ppermute | solution.py:801
  5.2 19.0 %copy-start.1 = (f32[1,40]{1,0:T(1,128)S(1)}, f32[1,40]{1,0:T(1,128)}, u32[]{:S(2)}) copy-start(f32[1,40]{1,0:T(1,128)} %param.27) | copy-start | bytes 484
  5.2 19.0 %copy-start.2 = (f32[1,40]{1,0:T(1,128)S(1)}, f32[1,40]{1,0:T(1,128)}, u32[]{:S(2)}) copy-start(f32[1,40]{1,0:T(1,128)} %param.26) | copy-start | bytes 484
  5.2 19.0 %copy-start.3 = (f32[1,40]{1,0:T(1,128)S(1)}, f32[1,40]{1,0:T(1,128)}, u32[]{:S(2)}) copy-start(f32[1,40]{1,0:T(1,128)} %param.25) | copy-start | bytes 484

commit v4 on v3

--- a/solution.py
+++ b/solution.py
@@ -34,7 +34,7 @@
 
 def mixer_kernel(
     live,
-    x_ref,
+    x_hbm,
     bcdt_ref,
     scaled_ref,
     scale_ref,
@@ -47,7 +47,7 @@
     cb_ref,
     bb_ref,
     hv_ref,
-    g_ref,
+    g_hbm,
     ss_ref,
     mask_s,
     l_s,
@@ -72,6 +72,10 @@
     rows_s,
     wz_s,
     z_s,
+    x_ref,
+    g_ref,
+    x_sem,
+    g_sem,
     rows_sem,
     wz_sem,
     send_sem,
@@ -125,8 +129,9 @@
     @pl.when(lax.axis_index("pipe") == live)
     def _():
         barrier = pltpu.get_barrier_semaphore()
+        x_copy = pltpu.make_async_copy(x_hbm, x_ref, x_sem)
+        x_copy.start()
         rows_copy = pltpu.make_async_copy(scaled_ref.at[pl.ds(HALO, rows)], rows_s, rows_sem)
-        rows_copy.start()
         gate_tile = span
 
         def gate_copy(n):
@@ -134,8 +139,6 @@
                 weight_zx.at[:, pl.ds(n * gate_tile, gate_tile)], wz_s.at[n], wz_sem.at[n]
             )
 
-        for n in range(width // gate_tile):
-            gate_copy(n).start()
         for distance in range(1, size):
             pl.semaphore_signal(
                 barrier,
@@ -261,6 +264,10 @@
             gate = jnp.dot(rows_s[...], wz_s[turn], preferred_element_type=f32)
             z_s[:, at] = (gate * widen(scale_ref[pl.ds(HALO, rows), :], group)).astype(bf16)
 
+        def leave_copy(turn):
+            lanes = pl.ds(pl.multiple_of(turn * span, span), span)
+            return pltpu.make_async_copy(g_ref.at[:, lanes], g_hbm.at[:, lanes], g_sem.at[turn])
+
         def leave(turn):
             lanes = pl.ds(pl.multiple_of(turn * span, span), span)
             pick = selector(turn * group, 2 * heads_pad, bf16)
@@ -283,6 +290,7 @@
                 g_ref[here, lanes] = (out * gg_ref[0:1, lanes]).astype(bf16)
                 if k < chunks - 1:
                     state = state * keeps[k : k + 1] + fresh_s[k, :, lanes]
+            leave_copy(turn).start()
 
         def send_half(half):
             for distance in range(1, size):
@@ -313,6 +321,10 @@
                 hop(back_s.at[me], inc_s.at[source], half, distance, bsend_sem, brecv_sem).wait_recv()
             pl.loop(*halves[half])(leave)
 
+        x_copy.wait()
+        rows_copy.start()
+        for n in range(width // gate_tile):
+            gate_copy(n).start()
         pl.loop(*halves[0])(enter)
         pl.semaphore_wait(barrier, size - 1)
         send_half(0)
@@ -329,6 +341,8 @@
                 scan_half(i)
         for half in range(2):
             leave_half(half)
+        for turn in range(turns):
+            leave_copy(turn).wait()
 
         for half in range(2):
             for distance in range(1, size):
@@ -358,8 +372,8 @@
             jax.ShapeDtypeStruct((rows, width), bf16),
             jax.ShapeDtypeStruct((rows, LANES), f32),
         ),
-        in_specs=[vmem, vmem, hbm, vmem, hbm] + [vmem] * 8,
-        out_specs=(vmem, vmem),
+        in_specs=[hbm, vmem, hbm, vmem, hbm] + [vmem] * 8,
+        out_specs=(hbm, vmem),
         scratch_shapes=[
             pltpu.VMEM((3, rows, LANES), f32),
             pltpu.VMEM((rows, heads_pad), f32),
@@ -384,6 +398,10 @@
             pltpu.VMEM((rows, features), bf16),
             pltpu.VMEM((width // gate_tile, features, gate_tile), bf16),
             pltpu.VMEM((rows, width), bf16),
+            pltpu.VMEM((rows + HALO, width), bf16),
+            pltpu.VMEM((rows, width), bf16),
+            pltpu.SemaphoreType.DMA,
+            pltpu.SemaphoreType.DMA((width // gate_tile,)),
             pltpu.SemaphoreType.DMA,
             pltpu.SemaphoreType.DMA((width // gate_tile,)),
             dma,
@@ -409,20 +427,24 @@
     take = lambda count: [next(refs) for _ in range(count)]
     sends_rows = out_live is None
     if out_live is not None:
-        gated_ref, squares_ref, weight_out = take(3)
-    (hidden_ref,) = take(1)
+        gated_hbm, squares_ref, weight_out = take(3)
+    (hidden_hbm,) = take(1)
+    hidden_ref = hidden_hbm
     if in_live is not None:
-        gain_ref, weight_zx, weight_bc, weight_dt = take(4)
+        gain_ref, weight_zx, bc_hbm, dt_hbm = take(4)
     if out_live is not None:
         (done_ref,) = take(1)
     if in_live is not None:
-        x_ref, small_ref, scaled_ref, scale_ref = take(4)
+        x_hbm, small_ref, scaled_hbm, scale_ref = take(4)
     if out_live is not None:
         wo_s, part_s, psend_s, precv_s, sqsend_s, sqrecv_s = take(6)
         wo_sem, psend_sem, precv_sem, sqsend_sem, sqrecv_sem = take(5)
+        gated_ref, hidden_ref, gated_sem, hidden_sem = take(4)
     if in_live is not None:
         rows_s, wz_s, acc_s, accb_s, squares_s = take(5)
         wz_sem, rsend_sem, rrecv_sem, hsend_sem, hrecv_sem = take(5)
+        x_ref, scaled_ref, weight_bc, weight_dt = take(4)
+        x_sem, scaled_sem, small_sem = take(3)
 
     tp = lax.axis_size("tp")
     shards = lax.axis_size("seq")
@@ -543,8 +565,20 @@
                     halo_copy(source, c, target).wait_send()
 
     def project():
+        smalls = [
+            pltpu.make_async_copy(bc_hbm, weight_bc, small_sem.at[0]),
+            pltpu.make_async_copy(dt_hbm, weight_dt, small_sem.at[1]),
+        ]
+        for copy in smalls:
+            copy.start()
         for c in range(pieces):
             weight_copy(c).start()
+
+        def scaled_copy(c):
+            return pltpu.make_async_copy(
+                scaled_ref.at[:, cols(c)], scaled_hbm.at[:, cols(c)], scaled_sem.at[c]
+            )
+
         for distance in range(1 if sends_rows else 0, tp):
             greet(pipe=from_live, tp=lax.rem(t - distance + tp, tp))
 
@@ -567,6 +601,11 @@
         total_rows = rows_s.shape[1]
         out_cols = x_ref.shape[1]
         tile = piece_width(out_cols)
+
+        def x_copy(n):
+            at = pl.ds(pl.multiple_of(n * tile, tile), tile)
+            return pltpu.make_async_copy(x_ref.at[:, at], x_hbm.at[:, at], x_sem.at[n])
+
         squares_s[...] = jnp.zeros_like(squares_s)
         for c in range(pieces):
             for distance in range(1 if sends_rows else 0, tp):
@@ -584,6 +623,10 @@
                 sums += square[:, i * LANES : (i + 1) * LANES]
             squares_s[...] += sums
             scaled_ref[:, cols(c)] = (values * gain_ref[0:1, cols(c)]).astype(bf16)
+            scaled_copy(c).start()
+            if c == 0:
+                for copy in smalls:
+                    copy.wait()
             last = c == pieces - 1
             if last:
                 mean = jnp.sum(squares_s[...], axis=1, keepdims=True) / features
@@ -616,18 +659,29 @@
                     value += acc_s[:, at]
                 if last:
                     x_ref[:, at] = (value * widen(scale_ref[...], tile // LANES)).astype(bf16)
+                    x_copy(n).start()
                 else:
                     acc_s[:, at] = value
 
             if not sends_rows:
                 mine = pl.ds(pl.multiple_of(HALO + t * count, HALO), count)
                 done_ref[:, cols(c)] = rows_s[c, mine, :]
+        for c in range(pieces):
+            scaled_copy(c).wait()
+        for n in range(out_cols // tile):
+            x_copy(n).wait()
         if sends_rows:
             drain_rows(hidden_ref)
 
+    def out_copy(c):
+        return pltpu.make_async_copy(weight_out.at[:, cols(c)], wo_s.at[c], wo_sem.at[c])
+
     def finish():
-        for c in range(pieces):
-            pltpu.make_async_copy(weight_out.at[:, cols(c)], wo_s.at[c], wo_sem.at[c]).start()
+        gated_copy = pltpu.make_async_copy(gated_hbm, gated_ref, gated_sem)
+        gated_copy.start()
+        for c in range(min(2, pieces)):
+            out_copy(c).start()
+        hidden_copy = pltpu.make_async_copy(hidden_hbm, hidden_ref, hidden_sem)
         for distance in range(1, tp):
             greet(tp=peer(distance))
         for target in range(tp):
@@ -640,7 +694,13 @@
                 preferred_element_type=f32,
             )
         for c in range(pieces):
-            pltpu.make_async_copy(weight_out.at[:, cols(c)], wo_s.at[c], wo_sem.at[c]).wait()
+            out_copy(c).wait()
+            if c + 2 < pieces:
+                out_copy(c + 2).start()
+            if c == 0:
+                gated_copy.wait()
+            if c == pieces - 1:
+                hidden_copy.start()
             for target in range(tp):
                 value = jnp.dot(
                     gated_ref[target * count : (target + 1) * count, :],
@@ -666,6 +726,7 @@
             precision=lax.Precision.HIGHEST,
             preferred_element_type=f32,
         )
+        hidden_copy.wait()
         scale = lax.rsqrt(sums / (gated_ref.shape[1] * tp) + epsilon)
         for c in range(pieces):
             total = part_s[c, t]
@@ -695,6 +756,9 @@
 
         @pl.when(idle)
         def _():
+            hidden_copy = pltpu.make_async_copy(hidden_hbm, hidden_ref, hidden_sem)
+            hidden_copy.start()
+            hidden_copy.wait()
             done_ref[...] = hidden_ref[...]
 
 
@@ -706,18 +770,19 @@
     vmem = pl.BlockSpec(memory_space=pltpu.VMEM)
     hbm = pl.BlockSpec(memory_space=pl.ANY)
     dma = pltpu.SemaphoreType.DMA
-    args, specs, outs, scratch = [], [], [], []
+    args, specs, outs, scratch, out_specs = [], [], [], [], []
     peers = max(1, tp - 1)
     if out_live is not None:
         args += out_args
-        specs += [vmem, vmem, hbm]
+        specs += [hbm, vmem, hbm]
     args.append(hidden)
-    specs.append(vmem)
+    specs.append(vmem if out_live is None else hbm)
     if in_live is not None:
         args += in_args
-        specs += [vmem, hbm, vmem, vmem]
+        specs += [vmem, hbm, hbm, hbm]
     if out_live is not None:
         outs.append(jax.ShapeDtypeStruct((count, features), bf16))
+        out_specs.append(vmem)
         width = out_args[2].shape[0]
         scratch += [
             pltpu.VMEM((pieces, width, piece), bf16),
@@ -731,11 +796,16 @@
             dma((pieces, peers)),
             dma((peers,)),
             dma((peers,)),
+            pltpu.VMEM((tp * count, width), bf16),
+            pltpu.VMEM((count, features), bf16),
+            dma,
+            dma,
         ]
     if in_live is not None:
         rows = HALO + tp * count
         wide = in_args[1].shape[1] // 2
         small = in_args[2].shape[1] + in_args[3].shape[1]
+        out_specs += [hbm, vmem, hbm, vmem]
         outs += [
             jax.ShapeDtypeStruct((rows, wide), bf16),
             jax.ShapeDtypeStruct((rows, small), f32),
@@ -753,6 +823,13 @@
             dma((pieces, tp)),
             dma((pieces, tp)),
             dma((pieces,)),
+            pltpu.VMEM((rows, wide), bf16),
+            pltpu.VMEM((rows, features), bf16),
+            pltpu.VMEM(in_args[2].shape, bf16),
+            pltpu.VMEM(in_args[3].shape, bf16),
+            dma((wide // piece_width(wide),)),
+            dma((pieces,)),
+            dma((2,)),
         ]
     sections = lax.axis_size("pipe")
     step = 0 if out_live is None else out_live + 1
@@ -760,7 +837,7 @@
         functools.partial(boundary_kernel, out_live, in_live),
         out_shape=tuple(outs),
         in_specs=specs,
-        out_specs=tuple([vmem] * len(outs)),
+        out_specs=tuple(out_specs),
         scratch_shapes=scratch,
         compiler_params=pltpu.CompilerParams(
             collective_id=sections + step,

time: 190 us -> 186 us (0.979)
  Pallas kernels: 162 us -> 157 us
    pallas_call x3, Pallas kernels: 123 us -> 121 us  [boundary(): pl.pallas_call(functools.partial(boundary_kernel, out_live, in_live), out...]
    pallas_call x2, Pallas kernels: 38.7 us -> 36.4 us  [mixer(): pl.pallas_call(functools.partial(mixer_kernel, live), out_shape=(jax.Shap...]
  transfers between devices with their start and end apart: 1 -> 1, of which waited for: 0 -> 0; matrix products, arithmetic and copies ran while one was open for 11% -> 11% of each run, Pallas kernels for 3% -> 1%
where the time goes in v4:
time: 186 us; the launch traced here: 185 us
  Pallas kernels  157 us (84%)
  local copies, waits for them, and re-layouts  23.6 us (13%)
  starting transfers between devices  3.16 us (2%)
    pallas_call x3, Pallas kernels, boundary(): pl.pallas_call(functools.partial(boundary_kernel, out_live, in_live), out...  121 us
    pallas_call x2, Pallas kernels, mixer(): pl.pallas_call(functools.partial(mixer_kernel, live), out_shape=(jax.Shap...  36.4 us
    unnamed x11, local copies, waits for them, and re-layouts  21.7 us
  transfers between devices with their start and end apart: 1, of which 0 were waited for; matrix products, arithmetic and copies ran while one was open for 11% of the time, Pallas kernels for 1%

profile of v4, /device:TPU:11, one launch (start us, length us, event | category | flops | bytes accessed | tf_op | source)
XLA Modules:
  0.0 185.2 jit_solution(8452517709194120921)
XLA Ops:
  0.0 0.7 convert_element_type.11.idr_ref
  0.7 0.0 copy-start
  0.7 0.1 fusion
  0.8 3.2 %collective-permute-start = (f32[16]{0:T(128)S(1)}, f32[16]{0:T(128)S(1)}, u32[]{:S(2)}, u32[]{:S(2)}) collective-permute-start(f32[16]{0:T(128)S(1)} %fusion), channel_id=1, source_target_pairs={{0,2},{2,4},{4,6},{6,8},{8,10},{10,12},{12,14},{1,3},{3,5},{5,7},{... | collective-permute-start | bytes 200 | tf_op jit(solution)/shard_map/ppermute | solution.py:878
  3.9 1.3 copy.16
  5.2 0.0 copy-start.1
  5.2 0.0 copy-start.2
  5.2 0.0 copy-start.3
  5.2 18.0 %copy.17 = bf16[320,8,2,2560]{3,1,2,0:T(8,128)(2,1)} copy(bf16[320,8,2,2560]{3,2,1,0:T(2,128)(2,1)} %bitcast.19) | data formatting | bytes 52428800
  23.2 1.0 pad.8.refs_4_.refs_7_
  24.2 0.0 copy-done.1
  24.2 0.0 copy-done.2
  24.2 0.0 copy-done.3
  24.2 0.6 select_maximum_fusion.hv_ref
  24.8 2.8 %boundary_0.1 = (bf16[528,2560]{1,0:T(8,128)(2,1)}, f32[528,384]{1,0:T(8,128)}, bf16[528,2560]{1,0:T(8,128)(2,1)}, f32[528,128]{1,0:T(8,128)}) custom-call(bf16[256,2560]{1,0:T(8,128)(2,1)} %bitcast.20, f32[1,2560]{1,0:T(1,128)} %refs_4_.1, bf16[2560,5120]{1,0:T(8,128)(2,1)} %bitcast.13, bf16[2560,256]{1,0:T(8,128)(2,1)} %bitcast.22, ...), custom_call_target="tpu_custom_call" | custom-call | tf_op jit(solution)/shard_map/boundary_0/pallas_call | solution.py:836
  27.6 0.0 collective-permute-done
  27.6 0.0 copy-done
  27.6 0.1 pad_maximum_fusion
  27.7 0.8 broadcast_in_dim.4.idc_ref
  28.5 3.0 %mixer_0.1 = (bf16[512,2560]{1,0:T(8,128)(2,1)}, f32[512,128]{1,0:T(8,128)}) custom-call(bf16[528,2560]{1,0:T(8,128)(2,1)} %get-tuple-element.18.x_hbm, f32[528,384]{1,0:T(8,128)} %get-tuple-element.19.bcdt_ref, bf16[528,2560]{1,0:T(8,128)(2,1)} %get-tuple-element.20.scaled_ref, f32[528,128]{1,0:T(8,128)} %get-tuple-element.21.scale_ref, ...), custom_call_target="tpu_custom_call" | custom-call | tf_op jit(solution)/shard_map/mixer_0/pallas_call | solution.py:369
  31.5 94.9 %boundary_1.1 = (bf16[256,2560]{1,0:T(8,128)(2,1)}, bf16[528,2560]{1,0:T(8,128)(2,1)}, f32[528,384]{1,0:T(8,128)}, bf16[528,2560]{1,0:T(8,128)(2,1)}, f32[528,128]{1,0:T(8,128)}) custom-call(bf16[512,2560]{1,0:T(8,128)(2,1)} %get-tuple-element.22.refs_0_, f32[512,128]{1,0:T(8,128)} %get-tuple-element.23.refs_1_, bf16[2560,2560]{1,0:T(8,128)(2,1)} %bitcast.17, ...), custom_call_target="tpu_custom_call" | custom-call | tf_op jit(solution)/shard_map/boundary_1/pallas_call | solution.py:836
  126.4 33.5 %mixer_1.1 = (bf16[512,2560]{1,0:T(8,128)(2,1)}, f32[512,128]{1,0:T(8,128)}) custom-call(bf16[528,2560]{1,0:T(8,128)(2,1)} %get-tuple-element.24.x_hbm, f32[528,384]{1,0:T(8,128)} %get-tuple-element.25.bcdt_ref, bf16[528,2560]{1,0:T(8,128)(2,1)} %get-tuple-element.26.scaled_ref, f32[528,128]{1,0:T(8,128)} %get-tuple-element.27.scale_ref, ...), custom_call_target="tpu_custom_call" | custom-call | tf_op jit(solution)/shard_map/mixer_1/pallas_call | solution.py:369
  159.8 22.9 %boundary_2.1 = bf16[256,2560]{1,0:T(8,128)(2,1)} custom-call(bf16[512,2560]{1,0:T(8,128)(2,1)} %get-tuple-element.28.refs_0_, f32[512,128]{1,0:T(8,128)} %get-tuple-element.29.refs_1_, bf16[2560,2560]{1,0:T(8,128)(2,1)} %bitcast.18, bf16[256,2560]{1,0:T(8,128)(2,1)} %get-tuple-element.30.refs_3_), custom_call_target="tpu_custom_call" | custom-call | tf_op jit(solution)/shard_map/boundary_2/pallas_call | solution.py:836
  182.8 2.5 %copy.19 = bf16[1,1,256,2560]{3,2,1,0:T(8,128)(2,1)} copy(bf16[1,1,256,2560]{3,2,1,0:T(8,128)(2,1)} %bitcast.24) | data formatting | bytes 2621440
  (1 shorter events, 0.0 us)
Async XLA Ops:
  0.7 26.9 %copy-start = (f32[1,512]{1,0:T(1,128)}, f32[1,512]{1,0:T(1,128)S(1)}, u32[]{:S(2)}) copy-start(f32[1,512]{1,0:T(1,128)S(1)} %convert_element_type.11.idr_ref) | copy-start | bytes 6148
  0.8 26.8 %collective-permute-start = (f32[16]{0:T(128)S(1)}, f32[16]{0:T(128)S(1)}, u32[]{:S(2)}, u32[]{:S(2)}) collective-permute-start(f32[16]{0:T(128)S(1)} %fusion), channel_id=1, source_target_pairs={{0,2},{2,4},{4,6},{6,8},{8,10},{10,12},{12,14},{1,3},{3,5},{5,7},{... | collective-permute-start | bytes 200 | tf_op jit(solution)/shard_map/ppermute | solution.py:878
  5.2 19.0 %copy-start.1 = (f32[1,40]{1,0:T(1,128)S(1)}, f32[1,40]{1,0:T(1,128)}, u32[]{:S(2)}) copy-start(f32[1,40]{1,0:T(1,128)} %param.27) | copy-start | bytes 484
  5.2 19.0 %copy-start.2 = (f32[1,40]{1,0:T(1,128)S(1)}, f32[1,40]{1,0:T(1,128)}, u32[]{:S(2)}) copy-start(f32[1,40]{1,0:T(1,128)} %param.26) | copy-start | bytes 484
  5.2 19.0 %copy-start.3 = (f32[1,40]{1,0:T(1,128)S(1)}, f32[1,40]{1,0:T(1,128)}, u32[]{:S(2)}) copy-start(f32[1,40]{1,0:T(1,128)} %param.25) | copy-start | bytes 484
